TPU v7x, 512 devices: a whole 4x8x8 slice. The times are simulated.
512 devices in a mesh: layer: 8 (over y_lo, core), row: 8 (over z), col: 8 (over y_hi, x).
Axes of the slice: x: 4, y: 8 (y_hi: 2, y_lo: 4; y = y_hi * 4 + y_lo), z: 8, core: 2. Of those that a mesh axis runs over, the one named last changes fastest.
Arguments:
- edge_weight: bfloat16 [8192, 8192], P('row', 'col'), may hold values from 0 to 1, as said below
Outputs:
- clustering: float32 [8, 1024], P('row', ('layer', 'col'))
Inputs may be any that keep to these rules, and one draw needn't show every extreme that they name: `edge_weight`: symmetric with a zero diagonal; every vertex v is linked to v - 1 and v + 1 (modulo 8192); an edge's entry lies in [0.2, 1], all other entries are 0.
All inputs are finite; a program needn't handle non-finite values.
Results may differ from a plain program's by a relative error of at most 0.0003.
Values may be sent and summed in bfloat16 or wider, within the bound.
No kernel may reach another device: no remote copies, remote signals or barrier semaphores. Data moves between devices by JAX's collectives and lax.ppermute only.
A program may use at most 64 MiB of HBM per device.

v0:
```python
import jax
import jax.numpy as jnp
from jax import lax
from jax.sharding import PartitionSpec as P

STRIPE = 128


def joined_along(tiles, dim):
    tiles = jnp.moveaxis(tiles, 0, dim)
    lengths = tiles.shape
    return tiles.reshape(*lengths[:dim], lengths[dim] * lengths[dim + 1], *lengths[dim + 2 :])


def from_everyone(value, axis):
    copies = jnp.broadcast_to(value, (lax.axis_size(axis), *value.shape))
    return lax.all_to_all(copies, axis, split_axis=0, concat_axis=0, tiled=True)


def gather_directly(value, axis, dim):
    return joined_along(from_everyone(value, axis), dim)


def split_up(value, dim, peers):
    lengths = value.shape
    tiles = value.reshape(*lengths[:dim], peers, lengths[dim] // peers, *lengths[dim + 1 :])
    return jnp.moveaxis(tiles, dim, 0)


def sent_and_summed(value, axis, dim):
    peers = lax.axis_size(axis)
    tiles = lax.all_to_all(split_up(value, dim, peers), axis, 0, 0, tiled=True)
    return jnp.sum(tiles, axis=0)


def local(edge_weight):
    layers = lax.axis_size("layer")
    layer_index = lax.axis_index("layer")
    row_count, col_count = edge_weight.shape
    row_global = lax.axis_index("row") * row_count + jnp.arange(row_count, dtype=jnp.int32)
    col_global = lax.axis_index("col") * col_count + jnp.arange(col_count, dtype=jnp.int32)
    lower = jnp.where(
        row_global[:, None] > col_global[None, :], edge_weight, jnp.zeros_like(edge_weight)
    )
    column_groups = lower.reshape(row_count, col_count // (STRIPE * layers), layers, STRIPE)
    left_local = lax.dynamic_index_in_dim(column_groups, layer_index, 2, keepdims=False).reshape(
        row_count, col_count // layers
    )
    row_groups = lower.reshape(row_count // (STRIPE * layers), layers, STRIPE, col_count)
    right_local = lax.dynamic_index_in_dim(row_groups, layer_index, 1, keepdims=False).reshape(
        row_count // layers, col_count
    )
    left_whole = gather_directly(left_local, "col", 1)
    right_whole = lax.all_gather(right_local, "row", axis=0, tiled=True)
    paths = jnp.dot(left_whole, right_whole, preferred_element_type=jnp.float32)
    triangles = jnp.sum(paths * lower, axis=1)
    degree = jnp.sum(jnp.where(left_local > 0, 1.0, 0.0).astype(jnp.float32), axis=1)
    tri_total, degree_total = (
        sent_and_summed(triangles, ("layer", "col"), 0),
        sent_and_summed(degree, ("layer", "col"), 0),
    )
    clustering = 2.0 * tri_total / jnp.maximum(degree_total * (degree_total - 1.0), 2.0)
    return clustering.reshape(1, -1)


def solution(mesh):
    placed = (P("row", "col"),)
    return jax.shard_map(
        local, mesh=mesh, in_specs=placed, out_specs=P("row", ("layer", "col")), check_vma=False
    )
```

profile of v0, /device:TPU:1, one launch (start us, length us, event | category | flops | bytes accessed | tf_op | source)
XLA Modules:
  0.0 114.4 jit_solution(18305877768996494363)
XLA Ops:
  6.5 4.0 %copy.8 = bf16[1024,1024]{0,1:T(8,128)(2,1)} copy(bf16[1024,1024]{1,0:T(8,128)(2,1)} %param.1) | data formatting | bytes 4194304 | tf_op args[0]
  10.5 2.1 %compare_select_fusion = bf16[1024,1024]{0,1:T(8,128)(2,1)S(1)} fusion(bf16[1024,1024]{0,1:T(8,128)(2,1)} %copy.8, s32[1024]{0:T(1024)S(1)} %get-tuple-element.6, s32[1024]{0:T(1024)S(1)} %get-tuple-element.5), kind=kLoop, calls=%fused_computation.1 | loop fusion | flops 2097152 | bytes 4202496 | tf_op jit(solution)/shard_map/jit(_where)/select_n | solution.py:42
  12.7 1.6 %broadcast_in_dim.17 = bf16[8,1024,128]{1,2,0:T(8,128)(2,1)} broadcast(bf16[1024,128]{0,1:T(8,128)(2,1)S(1)} %fusion.4), dimensions={1,2} | broadcast | bytes 2359296 | tf_op jit(solution)/shard_map/broadcast_in_dim | solution.py:16
  14.2 10.1 %all-to-all-start = ((bf16[8,1024,128]{1,2,0:T(8,128)(2,1)}), bf16[8,1024,128]{1,2,0:T(8,128)(2,1)}, u32[]{:S(2)}, u32[]{:S(2)}) async-start(bf16[8,1024,128]{1,2,0:T(8,128)(2,1)} %broadcast_in_dim.17), calls=%async_computation | async-start | bytes 4194304 | tf_op jit(solution)/shard_map/all_to_all | solution.py:17
  24.3 0.0 all-gather.3.cloned.1.call-start
  24.4 2.6 %copy.14 = bf16[1024,1024]{1,0:T(8,128)(2,1)} copy(bf16[1024,1024]{0,1:T(8,128)(2,1)S(1)} %compare_select_fusion) | data formatting | bytes 4194304 | tf_op jit(solution)/shard_map/reshape | solution.py:49
  27.0 1.7 %constant_dynamic-slice_fusion = bf16[1,1,128,1024]{3,2,1,0:T(8,128)(2,1)} fusion(bf16[1,8,128,1024]{3,2,1,0:T(8,128)(2,1)} %bitcast.21, s32[]{:T(128)S(6)} %select_n.15), kind=kLoop, calls=%fused_computation.9 | loop fusion | bytes 524292 | tf_op jit(solution)/shard_map/jit(dynamic_index_in_dim)/dynamic_slice | solution.py:50
  28.6 0.0 all-gather.3.cloned.1.call-update
  28.7 0.2 copy.15
  28.9 0.1 select_reduce_fusion
  29.0 0.7 all_to_all.18
  29.7 36.0 %all-to-all-done = bf16[8,1024,128]{1,2,0:T(8,128)(2,1)} async-done(((bf16[8,1024,128]{1,2,0:T(8,128)(2,1)}), bf16[8,1024,128]{1,2,0:T(8,128)(2,1)}, u32[]{:S(2)}, u32[]{:S(2)}) %all-to-all-start) | async-done | bytes 2097184 | tf_op jit(solution)/shard_map/all_to_all | solution.py:17
  65.7 16.5 %all-to-all-start.2 = ((f32[64,1,16]{2,1,0:T(1,128)}), f32[64,1,16]{2,1,0:T(1,128)S(1)}, u32[]{:S(2)}, u32[]{:S(2)}) async-start(f32[64,1,16]{2,1,0:T(1,128)} %bitcast.8), calls=%async_computation.2 | async-start | bytes 65536 | tf_op jit(solution)/shard_map/all_to_all | solution.py:32
  82.2 0.0 all-gather.3.cloned.1.call-done
  82.2 4.7 %multiply_reduce_fusion = f32[1024]{0:T(1024)S(1)} fusion(bf16[1024,1024]{0,1:T(8,128)(2,1)S(1)} %compare_select_fusion, bf16[1024,1024]{0,1:T(8,128)(2,1)} %bitcast.3, bf16[1,1,1024,1024]{3,2,1,0:T(8,128)(2,1)} %all-gather.3.cloned.1.call-done), kind=kOutput, calls=%fused_computation | convolution fusion | flops 2150628352 | bytes 6295552 | tf_op jit(solution)/shard_map/dot_general | solution.py:55
  86.8 0.7 all_to_all.16
  87.5 3.8 %all-to-all-done.2 = f32[64,1,16]{2,1,0:T(1,128)S(1)} async-done(((f32[64,1,16]{2,1,0:T(1,128)}), f32[64,1,16]{2,1,0:T(1,128)S(1)}, u32[]{:S(2)}, u32[]{:S(2)}) %all-to-all-start.2) | async-done | bytes 4128 | tf_op jit(solution)/shard_map/all_to_all | solution.py:32
  91.3 6.4 %all-to-all-start.1 = ((f32[64,1,16]{2,1,0:T(1,128)}), f32[64,1,16]{2,1,0:T(1,128)S(1)}, u32[]{:S(2)}, u32[]{:S(2)}) async-start(f32[64,1,16]{2,1,0:T(1,128)} %bitcast.6), calls=%async_computation.1 | async-start | bytes 65536 | tf_op jit(solution)/shard_map/all_to_all | solution.py:32
  97.7 0.1 reduce_sum.41
  97.8 9.1 %all-to-all-done.1 = f32[64,1,16]{2,1,0:T(1,128)S(1)} async-done(((f32[64,1,16]{2,1,0:T(1,128)}), f32[64,1,16]{2,1,0:T(1,128)S(1)}, u32[]{:S(2)}, u32[]{:S(2)}) %all-to-all-start.1) | async-done | bytes 4128 | tf_op jit(solution)/shard_map/all_to_all | solution.py:32
  106.9 0.1 reduce_sum.39
  107.0 0.5 fusion.2
  (3 shorter events, 0.1 us)
Async XLA Ops:
  14.2 51.4 %all-to-all-start = ((bf16[8,1024,128]{1,2,0:T(8,128)(2,1)}), bf16[8,1024,128]{1,2,0:T(8,128)(2,1)}, u32[]{:S(2)}, u32[]{:S(2)}) async-start(bf16[8,1024,128]{1,2,0:T(8,128)(2,1)} %broadcast_in_dim.17), calls=%async_computation | async-start | bytes 4194304 | tf_op jit(solution)/shard_map/all_to_all | solution.py:17
  24.3 57.8 %all-gather.3.cloned.1.call-start = ((), (), s32[]{:S(2)}) async-start(), calls=%async_computation.3 | async-start | bytes 2359296 | tf_op jit(solution)/shard_map/all_gather | solution.py:54
  65.7 25.7 %all-to-all-start.2 = ((f32[64,1,16]{2,1,0:T(1,128)}), f32[64,1,16]{2,1,0:T(1,128)S(1)}, u32[]{:S(2)}, u32[]{:S(2)}) async-start(f32[64,1,16]{2,1,0:T(1,128)} %bitcast.8), calls=%async_computation.2 | async-start | bytes 65536 | tf_op jit(solution)/shard_map/all_to_all | solution.py:32
  91.3 15.6 %all-to-all-start.1 = ((f32[64,1,16]{2,1,0:T(1,128)}), f32[64,1,16]{2,1,0:T(1,128)S(1)}, u32[]{:S(2)}, u32[]{:S(2)}) async-start(f32[64,1,16]{2,1,0:T(1,128)} %bitcast.6), calls=%async_computation.1 | async-start | bytes 65536 | tf_op jit(solution)/shard_map/all_to_all | solution.py:32
Sparse Core Ops, SparseCore 0:
  28.8 44.7 all-gather.2
where the time goes:
time: 115 us; the launch traced here: 114 us
  waiting for transfers between devices  48.9 us (43%)
  starting transfers between devices  33 us (29%)
  between operations  13.5 us (12%)
  local copies, waits for them, and re-layouts  11.3 us (10%)
  matrix products  4.66 us (4%)
  other arithmetic  2.98 us (3%)
    all_to_all x1, waiting for transfers between devices, from_everyone(): return lax.all_to_all(copies, axis, split_axis=0, concat_axis=0, tiled=True)  36 us
    all_to_all x2, starting transfers between devices, sent_and_summed(): tiles = lax.all_to_all(split_up(value, dim, peers), axis, 0, 0, tiled=True)  22.9 us
    all_to_all x2, waiting for transfers between devices, sent_and_summed(): tiles = lax.all_to_all(split_up(value, dim, peers), axis, 0, 0, tiled=True)  12.9 us
    all_to_all x1, starting transfers between devices, from_everyone(): return lax.all_to_all(copies, axis, split_axis=0, concat_axis=0, tiled=True)  10.1 us
    dot_general x1, matrix products, local(): paths = jnp.dot(left_whole, right_whole, preferred_element_type=jnp.float32)  4.66 us
    unnamed x2, local copies, waits for them, and re-layouts  4.12 us
    reshape x1, local copies, waits for them, and re-layouts, local(): lower.reshape(row_count // (STRIPE * layers), layers, STRIPE, col_count)  2.58 us
  transfers between devices with their start and end apart: 4, of which 3 were waited for; matrix products, arithmetic and copies ran while one was open for 8% of the time, Pallas kernels for 0%

commit v1 on v0

v1 whole, which is shorter than its diff:
```python
import functools

import jax
import jax.numpy as jnp
from jax import lax
from jax.experimental import pallas as pl
from jax.experimental.pallas import tpu as pltpu
from jax.sharding import PartitionSpec as P

F32 = jnp.float32
BLOCKS = 8
LABEL = [6, 0, 4, 2, 3, 5, 1, 7]
SLOPE = 5
DIAG_LAYER = [
    [3, 0, 7, 4, 6, 2, 1],
    [4, 6, 0, 2, 5, 3, 7],
    [5, 1, 4, 0, 2, 6, 3],
    [2, 1, 7, 4, 0, 6, 3],
    [0, 3, 4, 6, 7, 5, 2],
    [4, 7, 0, 2, 6, 3, 1],
    [3, 6, 1, 5, 0, 4, 2],
    [6, 2, 4, 1, 5, 0, 7],
]
ROWS_KIND, COLS_KIND, THIRD_KIND = 1, 2, 3
OWN_ROW, OWN_COL, OWN_DIAG = 1, 2, 3


def times(a, b):
    r = 0
    for i in range(3):
        if (b >> i) & 1:
            r ^= a << i
    for i in (4, 3):
        if (r >> i) & 1:
            r ^= 0b1011 << (i - 3)
    return r


def third_block(r, c):
    return LABEL.index(times(SLOPE, LABEL[r]) ^ times(SLOPE ^ 1, LABEL[c]))


def node(r, c):
    return r * BLOCKS + c


def device(layer, r, c):
    return layer * BLOCKS * BLOCKS + node(r, c)


def plan():
    col_pairs, row_pairs, kinds = [], [], [[0, 0]] * (BLOCKS * BLOCKS)
    for r in range(BLOCKS):
        for c in range(BLOCKS):
            if r == c:
                continue
            m = third_block(r, c)
            col_pairs.append((node(r, m), node(r, c)))
            row_pairs.append((node(m, c), node(r, c)))
            top = max(r, c, m)
            kinds[node(r, c)] = [{r: ROWS_KIND, c: COLS_KIND, m: THIRD_KIND}[top], top]
    diag_pairs, own = [], [0] * (BLOCKS**3)
    for d in range(BLOCKS):
        for layer in range(BLOCKS):
            own[device(layer, d, d)] = OWN_DIAG
        others = [o for o in range(BLOCKS) if o != d]
        for o, layer in zip(others, DIAG_LAYER[d]):
            target = device(layer, max(d, o), min(d, o))
            diag_pairs.append((device(layer, d, d), target))
            own[target] = OWN_COL if o > d else OWN_ROW
    return col_pairs, row_pairs, diag_pairs, kinds, own


def mm(a, b, dims=((1,), (0,))):
    return lax.dot_general(a, b, (dims, ((), ())), preferred_element_type=F32)


def fold_lanes(w):
    part = w[:, :128]
    for t in range(1, w.shape[1] // 128):
        part = part + w[:, 128 * t : 128 * (t + 1)]
    return jnp.sum(part.T, axis=0, keepdims=True)


def fold_rows(w):
    return jnp.sum(w.reshape(w.shape[0] // 8, 8, w.shape[1]), axis=0)


STEP = 256


def triple_kernel(info_ref, b_ref, x_ref, z_ref, out_ref):
    kind, top, layer = info_ref[0], info_ref[1], info_ref[2]
    n = b_ref.shape[0]
    out_ref[...] = jnp.zeros_like(out_ref)

    def put(vector, start):
        shape = (out_ref.shape[0], vector.shape[1])
        row = lax.broadcasted_iota(jnp.int32, shape, 0)
        spread = jnp.broadcast_to(vector, shape)
        out_ref[:, start : start + shape[1]] = jnp.where(row == top, spread, jnp.zeros_like(spread))

    @pl.when(kind == ROWS_KIND)
    def _():
        for s in range(0, n, STEP):
            w = mm(x_ref[s : s + STEP, :], z_ref[...]) * b_ref[s : s + STEP, :].astype(F32)
            put(fold_lanes(w), s)

    @pl.when(kind == COLS_KIND)
    def _():
        acc = jnp.zeros((8, n), F32)
        for s in range(0, n, STEP):
            w = mm(x_ref[s : s + STEP, :], z_ref[...]) * b_ref[s : s + STEP, :].astype(F32)
            acc = acc + fold_rows(w)
        put(jnp.sum(acc, axis=0, keepdims=True), 0)

    @pl.when(kind == THIRD_KIND)
    def _():
        width = x_ref.shape[1]
        acc = jnp.zeros((8, width), F32)
        for s in range(0, n, STEP):
            q = mm(b_ref[s : s + STEP, :], z_ref[...], ((1,), (1,)))
            acc = acc + fold_rows(q * x_ref[s : s + STEP, :].astype(F32))
        total = jnp.sum(acc, axis=0, keepdims=True)
        for k in range(n // width):
            @pl.when(layer == k)
            def _(k=k):
                put(total, k * width)


def own_kernel(info_ref, b_ref, u_ref, out_ref):
    own, layer, side = info_ref[0], info_ref[1], info_ref[2]
    n = b_ref.shape[0]
    h = n // 2
    width = n // BLOCKS
    out_ref[...] = jnp.zeros_like(out_ref)
    zero = jnp.zeros((), u_ref.dtype)

    def below(w, first_row):
        row = lax.broadcasted_iota(jnp.int32, w.shape, 0) + first_row
        col = lax.broadcasted_iota(jnp.int32, w.shape, 1)
        return jnp.where(row > col, w, jnp.zeros((), w.dtype))

    def halves():
        mix = u_ref[:, h:]
        row = lax.broadcasted_iota(jnp.int32, mix.shape, 0)
        col = lax.broadcasted_iota(jnp.int32, mix.shape, 1)
        return u_ref[:, :h], jnp.where(row < col, mix, zero), jnp.where(row > col, mix, zero)

    @pl.when(own == OWN_COL)
    def _():
        across, first, second = halves()
        for s in range(0, n, STEP):
            lo, hi = b_ref[s : s + STEP, :h], b_ref[s : s + STEP, h:]
            p_lo = mm(hi, across) + mm(lo, first)
            w = p_lo * lo.astype(F32) + mm(hi, second) * hi.astype(F32)
            out_ref[0:1, s : s + STEP] = fold_lanes(w)

    @pl.when(own == OWN_ROW)
    def _():
        across, first, second = halves()
        for s in range(0, h, STEP):
            p = mm(first[:, s : s + STEP], b_ref[:h, :], ((0,), (0,)))
            out_ref[0:1, s : s + STEP] = fold_lanes(p * b_ref[s : s + STEP, :].astype(F32))
        for s in range(0, h, STEP):
            p = mm(across[s : s + STEP, :], b_ref[:h, :]) + mm(second[s : s + STEP, :], b_ref[h:, :])
            out_ref[0:1, h + s : h + s + STEP] = fold_lanes(p * b_ref[h + s : h + s + STEP, :].astype(F32))

    for k in range(BLOCKS):
        cut = slice(k * width, (k + 1) * width)

        @pl.when(jnp.logical_and(layer == k, side >= 0))
        def _(cut=cut, k=k):
            rows = b_ref[cut, :]
            row = lax.broadcasted_iota(jnp.int32, rows.shape, 0) + k * width
            col = lax.broadcasted_iota(jnp.int32, rows.shape, 1)
            mine = jnp.logical_and(rows.astype(F32) > 0, jnp.logical_or(side > 0, row > col))
            out_ref[1:2, cut] = fold_lanes(jnp.where(mine, 1.0, 0.0).astype(F32))

        @pl.when(jnp.logical_and(layer == k, own == OWN_DIAG))
        def _(cut=cut, k=k):
            middle = below(b_ref[cut, :], k * width)
            for s in range(0, n, STEP):
                mine = below(b_ref[s : s + STEP, :], s)
                w = mm(mine[:, cut], middle) * mine.astype(F32)
                out_ref[0:1, s : s + STEP] = fold_lanes(w)


def vmem_call(kernel, out_shape, flops, nbytes, name):
    whole = pl.BlockSpec(memory_space=pltpu.VMEM)

    def call(info, *arrays):
        return pl.pallas_call(
            kernel,
            out_shape=out_shape,
            in_specs=[pl.BlockSpec(memory_space=pltpu.SMEM)] + [whole] * len(arrays),
            out_specs=whole,
            name=name,
            cost_estimate=pl.CostEstimate(flops=flops, bytes_accessed=nbytes, transcendentals=0),
            compiler_params=pltpu.CompilerParams(vmem_limit_bytes=32 * 1024 * 1024),
        )(info, *arrays)

    return call


def local(edge_weight):
    n = edge_weight.shape[0]
    width, half = n // BLOCKS, n // 2
    col_pairs, row_pairs, diag_pairs, kinds, own = plan()
    layer, r, c = (lax.axis_index(name).astype(jnp.int32) for name in ("layer", "row", "col"))
    here = r * BLOCKS + c
    kind = lax.dynamic_slice_in_dim(jnp.array(kinds, jnp.int32).reshape(-1), 2 * here, 2)
    own_kind = lax.dynamic_slice_in_dim(jnp.array(own, jnp.int32), layer * BLOCKS * BLOCKS + here, 1)
    triple_info = jnp.concatenate([kind, layer[None]])
    own_info = jnp.concatenate([own_kind, layer[None], (r - c)[None]])

    columns = lax.dynamic_slice_in_dim(edge_weight, layer * width, width, 1)
    rows = lax.dynamic_slice_in_dim(edge_weight, layer * width, width, 0)
    k = jnp.arange(half, dtype=jnp.int32)
    mix = jnp.where(k[:, None] > k[None, :], edge_weight[half:, half:], edge_weight[:half, :half])
    packed = jnp.concatenate([edge_weight[half:, :half], mix], axis=1)

    x = lax.ppermute(columns, ("row", "col"), col_pairs)
    z = lax.ppermute(rows, ("row", "col"), row_pairs)
    u = lax.ppermute(packed, ("layer", "row", "col"), diag_pairs)

    triples = vmem_call(
        triple_kernel, jax.ShapeDtypeStruct((BLOCKS, n), F32), 2 * n * n * width, 2 * n * n, "triples"
    )(triple_info, edge_weight, x, z)
    back = lax.all_to_all(triples, "row", 0, 0, tiled=True)
    mine = vmem_call(
        own_kernel, jax.ShapeDtypeStruct((2, n), F32), 3 * n * n * half, 4 * n * n, "own"
    )(own_info, edge_weight, u)
    total = jnp.sum(back, axis=0) + mine[0]
    peers = BLOCKS * BLOCKS
    sent = jnp.stack([total.reshape(peers, n // peers), mine[1].reshape(peers, n // peers)], axis=1)
    got = jnp.sum(lax.all_to_all(sent, ("layer", "col"), 0, 0, tiled=True), axis=0)
    degree = got[1]
    clustering = 2.0 * got[0] / jnp.maximum(degree * (degree - 1.0), 2.0)
    return clustering.reshape(1, -1)


def solution(mesh):
    placed = (P("row", "col"),)
    return jax.shard_map(
        local, mesh=mesh, in_specs=placed, out_specs=P("row", ("layer", "col")), check_vma=False
    )
```

time: 115 us -> 76 us (0.66)
  waiting for transfers between devices: 48.9 us -> 6.26 us
  blocking collectives: 0 us -> 23.1 us
  between operations: 13.5 us -> 0.11 us
  local copies, waits for them, and re-layouts: 11.3 us -> 2.35 us
  matrix products: 4.66 us -> 0 us
  starting transfers between devices: 33 us -> 36.8 us
  Pallas kernels: 0 us -> 3 us
    all_to_all x3 -> x1, waiting for transfers between devices: 48.9 us -> 6.26 us  [local(): back = lax.all_to_all(triples, 'row', 0, 0, tiled=True)]
    all_to_all x0 -> x1, blocking collectives: none -> 23.1 us  [local(): lax.all_to_all(sent, ('layer', 'col'), 0, 0, tiled=True)]
    ppermute x0 -> x3, starting transfers between devices: none -> 13.9 us  [the longest x1 12.5 us: local(): u = lax.ppermute(packed, ('layer', 'row', 'col'), diag_pairs)]
    all_to_all x3 -> x1, starting transfers between devices: 33 us -> 23 us  [local(): back = lax.all_to_all(triples, 'row', 0, 0, tiled=True)]
    dot_general x1 -> x0, matrix products: 4.66 us -> none  [local(): paths = jnp.dot(left_whole, right_whole, preferred_element_type=jnp.float32)]
    unnamed x2 -> x4, local copies, waits for them, and re-layouts: 4.12 us -> 0.01 us
    pallas_call x0 -> x2, Pallas kernels: none -> 3 us  [call(): pl.pallas_call(kernel, out_shape=out_shape, in_specs=[pl.BlockSpec(memory...]
    reshape x2 -> x0, local copies, waits for them, and re-layouts: 2.61 us -> none  [the longest x1 2.58 us: local(): lower.reshape(row_count // (STRIPE * layers), layers, STRIPE, col_count)]
  transfers between devices with their start and end apart: 4 -> 4, of which waited for: 3 -> 1; matrix products, arithmetic and copies ran while one was open for 8% -> 4% of each run, Pallas kernels for 0% -> 1%
where the time goes in v1:
time: 76 us; the launch traced here: 75.7 us
  starting transfers between devices  36.8 us (48%)
  blocking collectives  23.1 us (30%)
  waiting for transfers between devices  6.26 us (8%)
  other arithmetic  4.07 us (5%)
  Pallas kernels  3 us (4%)
  local copies, waits for them, and re-layouts  2.35 us (3%)
    all_to_all x1, blocking collectives, local(): lax.all_to_all(sent, ('layer', 'col'), 0, 0, tiled=True)  23.1 us
    all_to_all x1, starting transfers between devices, local(): back = lax.all_to_all(triples, 'row', 0, 0, tiled=True)  23 us
    ppermute x1, starting transfers between devices, local(): u = lax.ppermute(packed, ('layer', 'row', 'col'), diag_pairs)  12.5 us
    all_to_all x1, waiting for transfers between devices, local(): back = lax.all_to_all(triples, 'row', 0, 0, tiled=True)  6.26 us
    pallas_call x2, Pallas kernels, call(): pl.pallas_call(kernel, out_shape=out_shape, in_specs=[pl.BlockSpec(memory...  3 us
    slice x1, other arithmetic, local(): packed = jnp.concatenate([edge_weight[half:, :half], mix], axis=1)  1.6 us
  transfers between devices with their start and end apart: 4, of which 1 were waited for; matrix products, arithmetic and copies ran while one was open for 4% of the time, Pallas kernels for 1%

profile of v1, /device:TPU:1, one launch (start us, length us, event | category | flops | bytes accessed | tf_op | source)
XLA Modules:
  0.0 75.7 jit_solution(3565026265332176476)
XLA Ops:
  0.0 0.0 copy-start
  0.0 1.6 %fusion.3 = (bf16[512,512]{1,0:T(8,128)(2,1)S(1)}, bf16[512,512]{1,0:T(8,128)(2,1)S(1)}) fusion(bf16[1024,1024]{1,0:T(8,128)(2,1)} %b_ref.3), kind=kLoop, calls=%fused_computation.13 | loop fusion | flops 524288 | bytes 2621440 | tf_op jit(solution)/shard_map/slice | solution.py:221
  1.6 0.0 copy-start.1
  1.6 1.1 %pad_maximum_fusion = bf16[512,1024]{1,0:T(8,128)(2,1)} fusion(bf16[512,512]{1,0:T(8,128)(2,1)S(1)} %get-tuple-element.8, bf16[512,512]{1,0:T(8,128)(2,1)S(1)} %get-tuple-element.7), kind=kLoop, calls=%fused_computation | loop fusion | flops 2097152 | bytes 2097152 | tf_op jit(solution)/shard_map/concatenate | solution.py:221
  2.7 12.5 %collective-permute-start.2 = (bf16[512,1024]{1,0:T(8,128)(2,1)}, bf16[512,1024]{1,0:T(8,128)(2,1)}, u32[]{:S(2)}, u32[]{:S(2)}) collective-permute-start(bf16[512,1024]{1,0:T(8,128)(2,1)} %pad_maximum_fusion), channel_id=1, source_target_pairs={{192,200},{0,16},{448,472},{256,288},{384,424},{128,176},{64,120},... | collective-permute-start | bytes 3145736 | tf_op jit(solution)/shard_map/ppermute | solution.py:225
  15.2 0.0 copy-done
  15.3 0.1 constant_dynamic-slice_fusion.1
  15.3 0.7 collective-permute-start
  16.0 0.7 collective-permute-start.1
  16.7 1.2 %dynamic_slice.15 = s32[1]{0:T(128)} dynamic-slice(s32[512]{0:T(512)} %constant.37.clone, s32[]{:T(128)S(6)} %select_n.16), dynamic_slice_sizes={1} | dynamic-slice | bytes 12 | tf_op jit(solution)/shard_map/dynamic_slice | solution.py:213
  18.0 0.0 copy-done.1
  18.0 0.1 dynamic_slice.12
  18.1 0.1 pad_add_fusion.info_ref
  18.1 0.0 collective-permute-done.x_ref
  18.1 0.0 collective-permute-done.1.z_ref
  18.1 0.6 triples.1
  18.7 0.6 copy.8
  19.3 23.0 %all-to-all-start = ((f32[8,1,1024]{2,1,0:T(1,128)}), f32[8,1,1024]{2,1,0:T(1,128)S(1)}, u32[]{:S(2)}, u32[]{:S(2)}) async-start(f32[8,1,1024]{2,1,0:T(1,128)} %copy.8), calls=%async_computation | async-start | bytes 65536 | tf_op jit(solution)/shard_map/all_to_all | solution.py:230
  42.3 0.6 pad_add_fusion.1.info_ref
  42.9 6.3 %all-to-all-done = f32[8,1,1024]{2,1,0:T(1,128)S(1)} async-done(((f32[8,1,1024]{2,1,0:T(1,128)}), f32[8,1,1024]{2,1,0:T(1,128)S(1)}, u32[]{:S(2)}, u32[]{:S(2)}) %all-to-all-start) | async-done | bytes 32800 | tf_op jit(solution)/shard_map/all_to_all | solution.py:230
  49.2 0.1 reduce_sum.21
  49.3 0.0 collective-permute-done.2.u_ref
  49.3 2.4 %own.1 = f32[2,1024]{1,0:T(2,128)S(1)} custom-call(s32[3]{0:T(128)S(1)} %pad_add_fusion.1.info_ref, bf16[1024,1024]{1,0:T(8,128)(2,1)S(1)} %copy-done, bf16[512,1024]{1,0:T(8,128)(2,1)} %collective-permute-done.2.u_ref), custom_call_target="tpu_custom_call" | custom-call | flops 1610612736 | bytes 4194304 | tf_op jit(solution)/shard_map/own/pallas_call | solution.py:193
  51.8 0.1 stack_reshape_squeeze.3
  51.9 0.1 squeeze.2
  52.0 0.1 copy.9
  52.0 23.1 %all_to_all.14 = f32[64,2,16]{2,1,0:T(2,128)S(1)} all-to-all(f32[64,2,16]{2,1,0:T(2,128)S(1)} %copy.9), channel_id=1, replica_groups=mesh['layer'=8,'row'=8,'col'=8] {'layer','col'}, dimensions={0} | all-to-all | bytes 16384 | tf_op jit(solution)/shard_map/all_to_all | solution.py:237
  75.1 0.1 reduce_sum.22
  75.2 0.5 fusion.2
  (5 shorter events, 0.1 us)
Async XLA Ops:
  0.0 15.3 %copy-start = (bf16[1024,1024]{1,0:T(8,128)(2,1)S(1)}, bf16[1024,1024]{1,0:T(8,128)(2,1)}, u32[]{:S(2)}) copy-start(bf16[1024,1024]{1,0:T(8,128)(2,1)} %b_ref.3) | copy-start | bytes 6291460
  1.6 16.4 %copy-start.1 = (s32[128]{0:T(128)S(1)}, s32[128]{0:T(128)}, u32[]{:S(2)}) copy-start(s32[128]{0:T(128)} %constant.38) | copy-start | bytes 1540
  2.7 46.6 %collective-permute-start.2 = (bf16[512,1024]{1,0:T(8,128)(2,1)}, bf16[512,1024]{1,0:T(8,128)(2,1)}, u32[]{:S(2)}, u32[]{:S(2)}) collective-permute-start(bf16[512,1024]{1,0:T(8,128)(2,1)} %pad_maximum_fusion), channel_id=1, source_target_pairs={{192,200},{0,16},{448,472},{256,288},{384,424},{128,176},{64,120},... | collective-permute-start | bytes 3145736 | tf_op jit(solution)/shard_map/ppermute | solution.py:225
  15.3 2.8 %collective-permute-start = (bf16[1024,128]{1,0:T(8,128)(2,1)S(1)}, bf16[1024,128]{1,0:T(8,128)(2,1)S(1)}, u32[]{:S(2)}, u32[]{:S(2)}) collective-permute-start(bf16[1024,128]{1,0:T(8,128)(2,1)S(1)} %constant_dynamic-slice_fusion.1), channel_id=1, source_target_pairs={{4,1},{5,2},{1,3},{2,4},{6,5},{7,6},{3,7},{13,8},{8,10},{12,11},{1... | collective-permute-start | bytes 786440 | tf_op jit(solution)/shard_map/ppermute | solution.py:223
  16.0 2.1 %collective-permute-start.1 = (bf16[128,1024]{1,0:T(8,128)(2,1)S(1)}, bf16[128,1024]{1,0:T(8,128)(2,1)S(1)}, u32[]{:S(2)}, u32[]{:S(2)}) collective-permute-start(bf16[128,1024]{1,0:T(8,128)(2,1)S(1)} %constant_dynamic-slice_fusion), channel_id=1, source_target_pairs={{33,1},{42,2},{11,3},{20,4},{53,5},{62,6},{31,7},{40,8},{2,10},{35... | collective-permute-start | bytes 786440 | tf_op jit(solution)/shard_map/ppermute | solution.py:224
  19.3 29.8 %all-to-all-start = ((f32[8,1,1024]{2,1,0:T(1,128)}), f32[8,1,1024]{2,1,0:T(1,128)S(1)}, u32[]{:S(2)}, u32[]{:S(2)}) async-start(f32[8,1,1024]{2,1,0:T(1,128)} %copy.8), calls=%async_computation | async-start | bytes 65536 | tf_op jit(solution)/shard_map/all_to_all | solution.py:230

commit v2 on v1

--- a/solution.py
+++ b/solution.py
@@ -1,5 +1,3 @@
-import functools
-
 import jax
 import jax.numpy as jnp
 from jax import lax
@@ -7,10 +5,19 @@
 from jax.experimental.pallas import tpu as pltpu
 from jax.sharding import PartitionSpec as P
 
+
 F32 = jnp.float32
 BLOCKS = 8
-LABEL = [6, 0, 4, 2, 3, 5, 1, 7]
-SLOPE = 5
+THIRD = [
+    [0, 4, 3, 7, 2, 6, 1, 5],
+    [2, 1, 7, 6, 3, 0, 5, 4],
+    [6, 5, 2, 1, 7, 4, 3, 0],
+    [4, 0, 5, 3, 6, 1, 7, 2],
+    [5, 6, 1, 2, 4, 7, 0, 3],
+    [3, 7, 0, 4, 1, 5, 2, 6],
+    [7, 2, 4, 0, 5, 3, 6, 1],
+    [1, 3, 6, 5, 0, 2, 4, 7],
+]
 DIAG_LAYER = [
     [3, 0, 7, 4, 6, 2, 1],
     [4, 6, 0, 2, 5, 3, 7],
@@ -25,21 +32,6 @@
 OWN_ROW, OWN_COL, OWN_DIAG = 1, 2, 3
 
 
-def times(a, b):
-    r = 0
-    for i in range(3):
-        if (b >> i) & 1:
-            r ^= a << i
-    for i in (4, 3):
-        if (r >> i) & 1:
-            r ^= 0b1011 << (i - 3)
-    return r
-
-
-def third_block(r, c):
-    return LABEL.index(times(SLOPE, LABEL[r]) ^ times(SLOPE ^ 1, LABEL[c]))
-
-
 def node(r, c):
     return r * BLOCKS + c
 
@@ -54,7 +46,7 @@
         for c in range(BLOCKS):
             if r == c:
                 continue
-            m = third_block(r, c)
+            m = THIRD[r][c]
             col_pairs.append((node(r, m), node(r, c)))
             row_pairs.append((node(m, c), node(r, c)))
             top = max(r, c, m)
@@ -90,7 +82,8 @@
 
 
 def triple_kernel(info_ref, b_ref, x_ref, z_ref, out_ref):
-    kind, top, layer = info_ref[0], info_ref[1], info_ref[2]
+    here = lax.axis_index("row") * BLOCKS + lax.axis_index("col")
+    kind, top, layer = info_ref[2 * here], info_ref[2 * here + 1], lax.axis_index("layer")
     n = b_ref.shape[0]
     out_ref[...] = jnp.zeros_like(out_ref)
 
@@ -129,7 +122,8 @@
 
 
 def own_kernel(info_ref, b_ref, u_ref, out_ref):
-    own, layer, side = info_ref[0], info_ref[1], info_ref[2]
+    layer, r, c = (lax.axis_index(name) for name in ("layer", "row", "col"))
+    own, side = info_ref[(layer * BLOCKS + r) * BLOCKS + c], r - c
     n = b_ref.shape[0]
     h = n // 2
     width = n // BLOCKS
@@ -186,7 +180,7 @@
                 out_ref[0:1, s : s + STEP] = fold_lanes(w)
 
 
-def vmem_call(kernel, out_shape, flops, nbytes, name):
+def vmem_call(kernel, out_shape, flops, nbytes):
     whole = pl.BlockSpec(memory_space=pltpu.VMEM)
 
     def call(info, *arrays):
@@ -195,7 +189,6 @@
             out_shape=out_shape,
             in_specs=[pl.BlockSpec(memory_space=pltpu.SMEM)] + [whole] * len(arrays),
             out_specs=whole,
-            name=name,
             cost_estimate=pl.CostEstimate(flops=flops, bytes_accessed=nbytes, transcendentals=0),
             compiler_params=pltpu.CompilerParams(vmem_limit_bytes=32 * 1024 * 1024),
         )(info, *arrays)
@@ -203,33 +196,29 @@
     return call
 
 
-def local(edge_weight):
+def step(edge_weight):
     n = edge_weight.shape[0]
     width, half = n // BLOCKS, n // 2
     col_pairs, row_pairs, diag_pairs, kinds, own = plan()
-    layer, r, c = (lax.axis_index(name).astype(jnp.int32) for name in ("layer", "row", "col"))
-    here = r * BLOCKS + c
-    kind = lax.dynamic_slice_in_dim(jnp.array(kinds, jnp.int32).reshape(-1), 2 * here, 2)
-    own_kind = lax.dynamic_slice_in_dim(jnp.array(own, jnp.int32), layer * BLOCKS * BLOCKS + here, 1)
-    triple_info = jnp.concatenate([kind, layer[None]])
-    own_info = jnp.concatenate([own_kind, layer[None], (r - c)[None]])
+    layer = lax.axis_index("layer")
+    triple_info = jnp.array(kinds, jnp.int32).reshape(-1)
+    own_info = jnp.array(own, jnp.int32)
 
     columns = lax.dynamic_slice_in_dim(edge_weight, layer * width, width, 1)
     rows = lax.dynamic_slice_in_dim(edge_weight, layer * width, width, 0)
+    x = lax.ppermute(columns, ("row", "col"), col_pairs)
+    z = lax.ppermute(rows, ("row", "col"), row_pairs)
     k = jnp.arange(half, dtype=jnp.int32)
     mix = jnp.where(k[:, None] > k[None, :], edge_weight[half:, half:], edge_weight[:half, :half])
     packed = jnp.concatenate([edge_weight[half:, :half], mix], axis=1)
-
-    x = lax.ppermute(columns, ("row", "col"), col_pairs)
-    z = lax.ppermute(rows, ("row", "col"), row_pairs)
     u = lax.ppermute(packed, ("layer", "row", "col"), diag_pairs)
 
     triples = vmem_call(
-        triple_kernel, jax.ShapeDtypeStruct((BLOCKS, n), F32), 2 * n * n * width, 2 * n * n, "triples"
+        triple_kernel, jax.ShapeDtypeStruct((BLOCKS, n), F32), 2 * n * n * width, 2 * n * n
     )(triple_info, edge_weight, x, z)
     back = lax.all_to_all(triples, "row", 0, 0, tiled=True)
     mine = vmem_call(
-        own_kernel, jax.ShapeDtypeStruct((2, n), F32), 3 * n * n * half, 4 * n * n, "own"
+        own_kernel, jax.ShapeDtypeStruct((2, n), F32), 3 * n * n * half, 4 * n * n
     )(own_info, edge_weight, u)
     total = jnp.sum(back, axis=0) + mine[0]
     peers = BLOCKS * BLOCKS
@@ -243,5 +232,5 @@
 def solution(mesh):
     placed = (P("row", "col"),)
     return jax.shard_map(
-        local, mesh=mesh, in_specs=placed, out_specs=P("row", ("layer", "col")), check_vma=False
+        step, mesh=mesh, in_specs=placed, out_specs=P("row", ("layer", "col")), check_vma=False
     )

time: 76 us -> 72.2 us (0.950)
  blocking collectives: 23.1 us -> 52.6 us
  starting transfers between devices: 36.8 us -> 13 us
  waiting for transfers between devices: 6.26 us -> 0.01 us
  local copies, waits for them, and re-layouts: 2.35 us -> 0.45 us
    all_to_all x1 -> x2, blocking collectives: 23.1 us -> 52.6 us  [the longest x1 27.9 us: step(): lax.all_to_all(sent, ('layer', 'col'), 0, 0, tiled=True)]
    all_to_all x1 -> x0, starting transfers between devices: 23 us -> none  [local(): back = lax.all_to_all(triples, 'row', 0, 0, tiled=True)]
    all_to_all x1 -> x0, waiting for transfers between devices: 6.26 us -> none  [local(): back = lax.all_to_all(triples, 'row', 0, 0, tiled=True)]
    dynamic_slice x4 -> x2, local copies, waits for them, and re-layouts: 1.41 us -> 0.1 us  [the longest x1 0.08 us: step(): columns = lax.dynamic_slice_in_dim(edge_weight, layer * width, width, 1)]
    ppermute x3, starting transfers between devices: 13.9 us -> 13 us  [the longest x1 11.7 us: step(): u = lax.ppermute(packed, ('layer', 'row', 'col'), diag_pairs)]
    concatenate x3 -> x1, other arithmetic: 1.81 us -> 1.12 us  [step(): packed = jnp.concatenate([edge_weight[half:, :half], mix], axis=1)]
  transfers between devices with their start and end apart: 4 -> 3, of which waited for: 1 -> 0; matrix products, arithmetic and copies ran while one was open for 4% -> 0% of each run, Pallas kernels for 1% -> 1%
where the time goes in v2:
time: 72.2 us; the launch traced here: 72 us
  blocking collectives  52.6 us (73%)
  starting transfers between devices  13 us (18%)
  other arithmetic  3.37 us (5%)
  Pallas kernels  2.36 us (3%)
    all_to_all x1, blocking collectives, step(): lax.all_to_all(sent, ('layer', 'col'), 0, 0, tiled=True)  27.9 us
    all_to_all x1, blocking collectives, step(): back = lax.all_to_all(triples, 'row', 0, 0, tiled=True)  24.7 us
    ppermute x1, starting transfers between devices, step(): u = lax.ppermute(packed, ('layer', 'row', 'col'), diag_pairs)  11.7 us
    pallas_call x2, Pallas kernels, call(): pl.pallas_call(kernel, out_shape=out_shape, in_specs=[pl.BlockSpec(memory...  2.36 us
    slice x1, other arithmetic, step(): packed = jnp.concatenate([edge_weight[half:, :half], mix], axis=1)  1.6 us
  transfers between devices with their start and end apart: 3, of which 0 were waited for; matrix products, arithmetic and copies ran while one was open for 0% of the time, Pallas kernels for 1%

profile of v2, /device:TPU:1, one launch (start us, length us, event | category | flops | bytes accessed | tf_op | source)
XLA Modules:
  0.0 72.0 jit_solution(17294376211093593980)
XLA Ops:
  0.0 0.0 copy-start
  0.0 1.6 %fusion.3 = (bf16[512,512]{1,0:T(8,128)(2,1)S(1)}, bf16[512,512]{1,0:T(8,128)(2,1)S(1)}) fusion(bf16[1024,1024]{1,0:T(8,128)(2,1)} %b_ref.3), kind=kLoop, calls=%fused_computation.11 | loop fusion | flops 524288 | bytes 2621440 | tf_op jit(solution)/shard_map/slice | solution.py:213
  1.6 0.0 copy-start.1
  1.6 1.1 %pad_maximum_fusion = bf16[512,1024]{1,0:T(8,128)(2,1)} fusion(bf16[512,512]{1,0:T(8,128)(2,1)S(1)} %get-tuple-element.8, bf16[512,512]{1,0:T(8,128)(2,1)S(1)} %get-tuple-element.7), kind=kLoop, calls=%fused_computation | loop fusion | flops 2097152 | bytes 2097152 | tf_op jit(solution)/shard_map/concatenate | solution.py:213
  2.7 0.0 copy-start.2
  2.7 11.7 %collective-permute-start.2 = (bf16[512,1024]{1,0:T(8,128)(2,1)}, bf16[512,1024]{1,0:T(8,128)(2,1)S(1)}, u32[]{:S(2)}, u32[]{:S(2)}) collective-permute-start(bf16[512,1024]{1,0:T(8,128)(2,1)} %pad_maximum_fusion), channel_id=1, source_target_pairs={{192,200},{0,16},{448,472},{256,288},{384,424},{128,176},{64,120},... | collective-permute-start | bytes 3145736 | tf_op jit(solution)/shard_map/ppermute | solution.py:214
  14.4 0.0 copy-done
  14.4 0.1 constant_dynamic-slice_fusion.1
  14.5 0.7 collective-permute-start
  15.2 0.7 collective-permute-start.1
  15.9 0.0 collective-permute-done.x_ref
  15.9 0.0 collective-permute-done.1.z_ref
  15.9 0.0 copy-done.1
  15.9 0.6 shard_map.37
  16.6 24.7 %all_to_all.14 = f32[8,1,1024]{2,1,0:T(1,128)S(1)} all-to-all(f32[8,1,1024]{2,1,0:T(1,128)S(1)} %copy.8), channel_id=1, replica_groups=mesh['layer'=8,'row'=8,'col'=8] {'row'}, dimensions={0} | all-to-all | bytes 65536 | tf_op jit(solution)/shard_map/all_to_all | solution.py:219
  41.3 0.1 reduce_sum.21
  41.4 0.0 collective-permute-done.2.u_ref
  41.4 0.0 copy-done.2
  41.4 1.8 %shard_map.38 = f32[2,1024]{1,0:T(2,128)S(1)} custom-call(s32[512]{0:T(512)S(1)} %copy-done.2, bf16[1024,1024]{1,0:T(8,128)(2,1)S(1)} %copy-done, bf16[512,1024]{1,0:T(8,128)(2,1)S(1)} %collective-permute-done.2.u_ref), custom_call_target="tpu_custom_call" | custom-call | flops 1610612736 | bytes 4194304 | tf_op jit(solution)/shard_map/pallas_call | solution.py:187
  43.2 0.1 stack_reshape_squeeze.3
  43.3 0.1 squeeze.2
  43.4 0.1 copy.9
  43.5 27.9 %all_to_all.15 = f32[64,2,16]{2,1,0:T(2,128)S(1)} all-to-all(f32[64,2,16]{2,1,0:T(2,128)S(1)} %copy.9), channel_id=1, replica_groups=mesh['layer'=8,'row'=8,'col'=8] {'layer','col'}, dimensions={0} | all-to-all | bytes 16384 | tf_op jit(solution)/shard_map/all_to_all | solution.py:226
  71.4 0.1 reduce_sum.22
  71.5 0.5 fusion.2
  (6 shorter events, 0.1 us)
Async XLA Ops:
  0.0 14.4 %copy-start = (bf16[1024,1024]{1,0:T(8,128)(2,1)S(1)}, bf16[1024,1024]{1,0:T(8,128)(2,1)}, u32[]{:S(2)}) copy-start(bf16[1024,1024]{1,0:T(8,128)(2,1)} %b_ref.3) | copy-start | bytes 6291460
  1.6 14.3 %copy-start.1 = (s32[128]{0:T(128)S(1)}, s32[128]{0:T(128)}, u32[]{:S(2)}) copy-start(s32[128]{0:T(128)} %constant.25.info_ref) | copy-start | bytes 1540
  2.7 38.7 %copy-start.2 = (s32[512]{0:T(512)S(1)}, s32[512]{0:T(512)}, u32[]{:S(2)}) copy-start(s32[512]{0:T(512)} %constant.24.clone.info_ref) | copy-start | bytes 6148
  2.7 38.7 %collective-permute-start.2 = (bf16[512,1024]{1,0:T(8,128)(2,1)}, bf16[512,1024]{1,0:T(8,128)(2,1)S(1)}, u32[]{:S(2)}, u32[]{:S(2)}) collective-permute-start(bf16[512,1024]{1,0:T(8,128)(2,1)} %pad_maximum_fusion), channel_id=1, source_target_pairs={{192,200},{0,16},{448,472},{256,288},{384,424},{128,176},{64,120},... | collective-permute-start | bytes 3145736 | tf_op jit(solution)/shard_map/ppermute | solution.py:214
  14.5 1.4 %collective-permute-start = (bf16[1024,128]{1,0:T(8,128)(2,1)S(1)}, bf16[1024,128]{1,0:T(8,128)(2,1)S(1)}, u32[]{:S(2)}, u32[]{:S(2)}) collective-permute-start(bf16[1024,128]{1,0:T(8,128)(2,1)S(1)} %constant_dynamic-slice_fusion.1), channel_id=1, source_target_pairs={{4,1},{3,2},{7,3},{2,4},{6,5},{1,6},{5,7},{10,8},{15,10},{14,11},{... | collective-permute-start | bytes 786440 | tf_op jit(solution)/shard_map/ppermute | solution.py:209
  15.2 0.7 collective-permute-start.1

commit v3 on v2

--- a/solution.py
+++ b/solution.py
@@ -9,27 +9,37 @@
 F32 = jnp.float32
 BLOCKS = 8
 THIRD = [
-    [0, 4, 3, 7, 2, 6, 1, 5],
-    [2, 1, 7, 6, 3, 0, 5, 4],
-    [6, 5, 2, 1, 7, 4, 3, 0],
-    [4, 0, 5, 3, 6, 1, 7, 2],
-    [5, 6, 1, 2, 4, 7, 0, 3],
-    [3, 7, 0, 4, 1, 5, 2, 6],
-    [7, 2, 4, 0, 5, 3, 6, 1],
-    [1, 3, 6, 5, 0, 2, 4, 7],
+    [0, 3, 6, 4, 2, 7, 5, 1],
+    [4, 1, 0, 5, 3, 6, 7, 2],
+    [5, 6, 2, 1, 7, 4, 3, 0],
+    [2, 7, 5, 3, 6, 0, 1, 4],
+    [7, 5, 1, 2, 4, 3, 0, 6],
+    [1, 2, 7, 6, 0, 5, 4, 3],
+    [3, 0, 4, 7, 1, 2, 6, 5],
+    [6, 4, 3, 0, 5, 1, 2, 7],
 ]
-DIAG_LAYER = [
-    [3, 0, 7, 4, 6, 2, 1],
-    [4, 6, 0, 2, 5, 3, 7],
-    [5, 1, 4, 0, 2, 6, 3],
-    [2, 1, 7, 4, 0, 6, 3],
-    [0, 3, 4, 6, 7, 5, 2],
-    [4, 7, 0, 2, 6, 3, 1],
-    [3, 6, 1, 5, 0, 4, 2],
-    [6, 2, 4, 1, 5, 0, 7],
+PACKED_LAYER = [
+    [-1, 5, 2, 6, 1, 3, 7, 4],
+    [3, -1, 4, 1, 6, 2, 7, 5],
+    [6, 0, -1, 1, 2, 4, 7, 3],
+    [1, 6, 5, -1, 0, 7, 4, 2],
+    [-1, -1, 5, 1, -1, 0, 6, 3],
+    [-1, 7, -1, 0, 5, -1, 6, 1],
+    [-1, 4, 1, -1, 7, 0, -1, 2],
+    [-1, 1, 6, -1, 4, 7, 0, -1],
 ]
+GRAM_LAYERS = {
+    (4, 0): (1, 4),
+    (4, 1): (3, 7),
+    (5, 0): (2, 4),
+    (5, 2): (0, 5),
+    (6, 0): (1, 4),
+    (6, 3): (3, 7),
+    (7, 0): (3, 5),
+    (7, 3): (0, 6),
+}
 ROWS_KIND, COLS_KIND, THIRD_KIND = 1, 2, 3
-OWN_ROW, OWN_COL, OWN_DIAG = 1, 2, 3
+OWN_ROW, OWN_COL, OWN_DIAG, OWN_GRAM = 1, 2, 3, 4
 
 
 def node(r, c):
@@ -55,11 +65,16 @@
     for d in range(BLOCKS):
         for layer in range(BLOCKS):
             own[device(layer, d, d)] = OWN_DIAG
-        others = [o for o in range(BLOCKS) if o != d]
-        for o, layer in zip(others, DIAG_LAYER[d]):
-            target = device(layer, max(d, o), min(d, o))
-            diag_pairs.append((device(layer, d, d), target))
-            own[target] = OWN_COL if o > d else OWN_ROW
+        for o in range(BLOCKS):
+            layer = PACKED_LAYER[d][o]
+            if layer >= 0:
+                target = device(layer, max(d, o), min(d, o))
+                diag_pairs.append((device(layer, d, d), target))
+                own[target] = OWN_COL if o > d else OWN_ROW
+            for layer in GRAM_LAYERS.get((d, o), ()):
+                target = device(layer, d, d)
+                diag_pairs.append((device(layer, o, d), target))
+                own[target] = OWN_GRAM
     return col_pairs, row_pairs, diag_pairs, kinds, own
 
 
@@ -171,13 +186,89 @@
             mine = jnp.logical_and(rows.astype(F32) > 0, jnp.logical_or(side > 0, row > col))
             out_ref[1:2, cut] = fold_lanes(jnp.where(mine, 1.0, 0.0).astype(F32))
 
-        @pl.when(jnp.logical_and(layer == k, own == OWN_DIAG))
+        @pl.when(jnp.logical_and(layer == k, side == 0))
         def _(cut=cut, k=k):
             middle = below(b_ref[cut, :], k * width)
             for s in range(0, n, STEP):
                 mine = below(b_ref[s : s + STEP, :], s)
                 w = mm(mine[:, cut], middle) * mine.astype(F32)
                 out_ref[0:1, s : s + STEP] = fold_lanes(w)
+
+
+    @pl.when(own == OWN_GRAM)
+    def _():
+        for s in range(0, n, STEP):
+            e = s + STEP
+            g = mm(u_ref[:, s:e], u_ref[:, :e], ((0,), (0,)))
+            out_ref[0:1, s:e] += fold_lanes(g * below(b_ref[s:e, :e], s).astype(F32))
+
+
+def cut_kernel(b_ref, columns_ref, rows_ref, sems):
+    width = columns_ref.shape[1]
+    start = pl.multiple_of(lax.axis_index("layer") * width, width)
+    copies = (
+        pltpu.make_async_copy(b_ref.at[:, pl.ds(start, width)], columns_ref, sems.at[0]),
+        pltpu.make_async_copy(b_ref.at[pl.ds(start, width), :], rows_ref, sems.at[1]),
+    )
+    for copy in copies:
+        copy.start()
+    for copy in copies:
+        copy.wait()
+
+
+def pack_kernel(b_ref, out_ref):
+    h = out_ref.shape[0]
+    diagonal = lax.axis_index("row") == lax.axis_index("col")
+    second = lax.axis_index("layer") >= BLOCKS // 2
+
+    @pl.when(diagonal)
+    def _():
+        out_ref[:, :h] = b_ref[h:, :h]
+        row = lax.broadcasted_iota(jnp.int32, (h, h), 0)
+        col = lax.broadcasted_iota(jnp.int32, (h, h), 1)
+        out_ref[:, h:] = jnp.where(row > col, b_ref[h:, h:], b_ref[:h, :h])
+
+    @pl.when(jnp.logical_not(diagonal))
+    def _():
+        @pl.when(second)
+        def _():
+            out_ref[...] = b_ref[h:, :]
+
+        @pl.when(jnp.logical_not(second))
+        def _():
+            out_ref[...] = b_ref[:h, :]
+
+
+def cut(edge_weight):
+    n = edge_weight.shape[0]
+    width = n // BLOCKS
+    return pl.pallas_call(
+        cut_kernel,
+        out_shape=(
+            jax.ShapeDtypeStruct((n, width), edge_weight.dtype),
+            jax.ShapeDtypeStruct((width, n), edge_weight.dtype),
+        ),
+        in_specs=[pl.BlockSpec(memory_space=pltpu.HBM)],
+        out_specs=(pl.BlockSpec(memory_space=pltpu.VMEM), pl.BlockSpec(memory_space=pltpu.VMEM)),
+        scratch_shapes=[pltpu.SemaphoreType.DMA((2,))],
+        name="cut",
+        cost_estimate=pl.CostEstimate(flops=0, bytes_accessed=4 * n * width, transcendentals=0),
+        compiler_params=pltpu.CompilerParams(vmem_limit_bytes=8 * 1024 * 1024),
+    )(edge_weight)
+
+
+def pack(edge_weight):
+    n = edge_weight.shape[0]
+    whole = pl.BlockSpec(memory_space=pltpu.VMEM)
+    return pl.pallas_call(
+        pack_kernel,
+        out_shape=jax.ShapeDtypeStruct((n // 2, n), edge_weight.dtype),
+        in_specs=[whole],
+        out_specs=whole,
+        name="pack",
+        cost_estimate=pl.CostEstimate(flops=0, bytes_accessed=2 * n * n, transcendentals=0),
+        compiler_params=pltpu.CompilerParams(vmem_limit_bytes=16 * 1024 * 1024),
+    )(edge_weight)
 
 
 def vmem_call(kernel, out_shape, flops, nbytes):
@@ -200,17 +291,13 @@
     n = edge_weight.shape[0]
     width, half = n // BLOCKS, n // 2
     col_pairs, row_pairs, diag_pairs, kinds, own = plan()
-    layer = lax.axis_index("layer")
     triple_info = jnp.array(kinds, jnp.int32).reshape(-1)
     own_info = jnp.array(own, jnp.int32)
 
-    columns = lax.dynamic_slice_in_dim(edge_weight, layer * width, width, 1)
-    rows = lax.dynamic_slice_in_dim(edge_weight, layer * width, width, 0)
+    columns, rows = cut(edge_weight)
     x = lax.ppermute(columns, ("row", "col"), col_pairs)
     z = lax.ppermute(rows, ("row", "col"), row_pairs)
-    k = jnp.arange(half, dtype=jnp.int32)
-    mix = jnp.where(k[:, None] > k[None, :], edge_weight[half:, half:], edge_weight[:half, :half])
-    packed = jnp.concatenate([edge_weight[half:, :half], mix], axis=1)
+    packed = pack(edge_weight)
     u = lax.ppermute(packed, ("layer", "row", "col"), diag_pairs)
 
     triples = vmem_call(

time: 72.2 us -> 74.4 us (1.030)
  other arithmetic: 3.37 us -> 0.65 us
  blocking collectives: 52.6 us -> 54.2 us
  local copies, waits for them, and re-layouts: 0.45 us -> 1.94 us
  starting transfers between devices: 13 us -> 13.9 us
  Pallas kernels: 2.36 us -> 3.23 us
    all_to_all x1, blocking collectives: 24.7 us -> 32.9 us  [step(): back = lax.all_to_all(triples, 'row', 0, 0, tiled=True)]
    all_to_all x1, blocking collectives: 27.9 us -> 21.3 us  [step(): lax.all_to_all(sent, ('layer', 'col'), 0, 0, tiled=True)]
    slice x1 -> x0, other arithmetic: 1.6 us -> none  [step(): packed = jnp.concatenate([edge_weight[half:, :half], mix], axis=1)]
    unnamed x6 -> x8, local copies, waits for them, and re-layouts: 0.01 us -> 1.6 us
    concatenate x1 -> x0, other arithmetic: 1.12 us -> none  [step(): packed = jnp.concatenate([edge_weight[half:, :half], mix], axis=1)]
    ppermute x1, starting transfers between devices: 11.7 us -> 12.5 us  [step(): u = lax.ppermute(packed, ('layer', 'row', 'col'), diag_pairs)]
where the time goes in v3:
time: 74.4 us; the launch traced here: 74.1 us
  blocking collectives  54.2 us (73%)
  starting transfers between devices  13.9 us (19%)
  Pallas kernels  3.23 us (4%)
  local copies, waits for them, and re-layouts  1.94 us (3%)
    all_to_all x1, blocking collectives, step(): back = lax.all_to_all(triples, 'row', 0, 0, tiled=True)  32.9 us
    all_to_all x1, blocking collectives, step(): lax.all_to_all(sent, ('layer', 'col'), 0, 0, tiled=True)  21.3 us
    ppermute x1, starting transfers between devices, step(): u = lax.ppermute(packed, ('layer', 'row', 'col'), diag_pairs)  12.5 us
    pallas_call x2, Pallas kernels, call(): pl.pallas_call(kernel, out_shape=out_shape, in_specs=[pl.BlockSpec(memory...  3.03 us
    unnamed x8, local copies, waits for them, and re-layouts  1.6 us
  transfers between devices with their start and end apart: 3, of which 0 were waited for; matrix products, arithmetic and copies ran while one was open for 0% of the time, Pallas kernels for 1%

profile of v3, /device:TPU:1, one launch (start us, length us, event | category | flops | bytes accessed | tf_op | source)
XLA Modules:
  0.0 74.1 jit_solution(17300792928655121902)
XLA Ops:
  0.0 0.0 copy-start
  0.0 1.6 %copy-done = bf16[1024,1024]{1,0:T(8,128)(2,1)S(1)} copy-done((bf16[1024,1024]{1,0:T(8,128)(2,1)S(1)}, bf16[1024,1024]{1,0:T(8,128)(2,1)}, u32[]{:S(2)}) %copy-start) | copy-done | bytes 2097176
  1.6 0.0 copy-start.1
  1.6 0.0 copy-start.2
  1.6 0.1 pack.1
  1.7 0.0 copy-start.3
  1.7 12.5 %collective-permute-start.2 = (bf16[512,1024]{1,0:T(8,128)(2,1)S(1)}, bf16[512,1024]{1,0:T(8,128)(2,1)}, u32[]{:S(2)}, u32[]{:S(2)}) collective-permute-start(bf16[512,1024]{1,0:T(8,128)(2,1)S(1)} %pack.1), channel_id=1, source_target_pairs={{320,328},{128,144},{384,408},{64,96},{192,232},{448,496},{256,312... | collective-permute-start | bytes 3145736 | tf_op jit(solution)/shard_map/ppermute | solution.py:301
  14.3 0.1 cut.1
  14.4 0.7 collective-permute-start
  15.1 0.7 collective-permute-start.1
  15.7 0.0 collective-permute-done.x_ref
  15.8 0.0 collective-permute-done.1.z_ref
  15.8 0.0 copy-done.1
  15.8 0.0 copy-done.2
  15.8 0.6 shard_map.37
  16.4 32.9 %all_to_all.14 = f32[8,1,1024]{2,1,0:T(1,128)S(1)} all-to-all(f32[8,1,1024]{2,1,0:T(1,128)S(1)} %copy.8), channel_id=1, replica_groups=mesh['layer'=8,'row'=8,'col'=8] {'row'}, dimensions={0} | all-to-all | bytes 65536 | tf_op jit(solution)/shard_map/all_to_all | solution.py:306
  49.4 0.1 reduce_sum.21
  49.5 0.0 collective-permute-done.2.u_ref
  49.5 0.0 copy-done.3
  49.5 2.5 %shard_map.38 = f32[2,1024]{1,0:T(2,128)S(1)} custom-call(s32[512]{0:T(512)S(1)} %copy-done.3, bf16[1024,1024]{1,0:T(8,128)(2,1)S(1)} %copy-done.1, bf16[512,1024]{1,0:T(8,128)(2,1)} %collective-permute-done.2.u_ref), custom_call_target="tpu_custom_call" | custom-call | flops 1610612736 | bytes 4194304 | tf_op jit(solution)/shard_map/pallas_call | solution.py:278
  52.0 0.1 stack_reshape_squeeze.3
  52.0 0.1 squeeze.2
  52.1 0.1 copy.9
  52.2 21.3 %all_to_all.15 = f32[64,2,16]{2,1,0:T(2,128)S(1)} all-to-all(f32[64,2,16]{2,1,0:T(2,128)S(1)} %copy.9), channel_id=1, replica_groups=mesh['layer'=8,'row'=8,'col'=8] {'layer','col'}, dimensions={0} | all-to-all | bytes 16384 | tf_op jit(solution)/shard_map/all_to_all | solution.py:313
  73.5 0.1 reduce_sum.22
  73.6 0.5 fusion.1
  (5 shorter events, 0.1 us)
Async XLA Ops:
  0.0 1.6 %copy-start = (bf16[1024,1024]{1,0:T(8,128)(2,1)S(1)}, bf16[1024,1024]{1,0:T(8,128)(2,1)}, u32[]{:S(2)}) copy-start(bf16[1024,1024]{1,0:T(8,128)(2,1)} %b_ref.7) | copy-start | bytes 6291460
  1.6 14.2 %copy-start.1 = (bf16[1024,1024]{1,0:T(8,128)(2,1)S(1)}, bf16[1024,1024]{1,0:T(8,128)(2,1)}, u32[]{:S(2)}) copy-start(bf16[1024,1024]{1,0:T(8,128)(2,1)} %b_ref.7) | copy-start | bytes 6291460
  1.6 14.2 %copy-start.2 = (s32[128]{0:T(128)S(1)}, s32[128]{0:T(128)}, u32[]{:S(2)}) copy-start(s32[128]{0:T(128)} %constant.13.info_ref) | copy-start | bytes 1540
  1.7 47.8 %copy-start.3 = (s32[512]{0:T(512)S(1)}, s32[512]{0:T(512)}, u32[]{:S(2)}) copy-start(s32[512]{0:T(512)} %constant.12.clone.info_ref) | copy-start | bytes 6148
  1.7 47.7 %collective-permute-start.2 = (bf16[512,1024]{1,0:T(8,128)(2,1)S(1)}, bf16[512,1024]{1,0:T(8,128)(2,1)}, u32[]{:S(2)}, u32[]{:S(2)}) collective-permute-start(bf16[512,1024]{1,0:T(8,128)(2,1)S(1)} %pack.1), channel_id=1, source_target_pairs={{320,328},{128,144},{384,408},{64,96},{192,232},{448,496},{256,312... | collective-permute-start | bytes 3145736 | tf_op jit(solution)/shard_map/ppermute | solution.py:301
  14.4 1.4 %collective-permute-start = (bf16[1024,128]{1,0:T(8,128)(2,1)S(1)}, bf16[1024,128]{1,0:T(8,128)(2,1)S(1)}, u32[]{:S(2)}, u32[]{:S(2)}) collective-permute-start(bf16[1024,128]{1,0:T(8,128)(2,1)S(1)} %get-tuple-element.7), channel_id=1, source_target_pairs={{3,1},{6,2},{4,3},{2,4},{7,5},{5,6},{1,7},{12,8},{8,10},{13,11},{1... | collective-permute-start | bytes 786440 | tf_op jit(solution)/shard_map/ppermute | solution.py:298
  15.1 0.7 collective-permute-start.1

commit v4 on v3

--- a/solution.py
+++ b/solution.py
@@ -18,28 +18,11 @@
     [3, 0, 4, 7, 1, 2, 6, 5],
     [6, 4, 3, 0, 5, 1, 2, 7],
 ]
-PACKED_LAYER = [
-    [-1, 5, 2, 6, 1, 3, 7, 4],
-    [3, -1, 4, 1, 6, 2, 7, 5],
-    [6, 0, -1, 1, 2, 4, 7, 3],
-    [1, 6, 5, -1, 0, 7, 4, 2],
-    [-1, -1, 5, 1, -1, 0, 6, 3],
-    [-1, 7, -1, 0, 5, -1, 6, 1],
-    [-1, 4, 1, -1, 7, 0, -1, 2],
-    [-1, 1, 6, -1, 4, 7, 0, -1],
-]
-GRAM_LAYERS = {
-    (4, 0): (1, 4),
-    (4, 1): (3, 7),
-    (5, 0): (2, 4),
-    (5, 2): (0, 5),
-    (6, 0): (1, 4),
-    (6, 3): (3, 7),
-    (7, 0): (3, 5),
-    (7, 3): (0, 6),
-}
+GRAM = {4: (0, 1), 5: (0, 2), 6: (0, 3), 7: (0, 3)}
+PIECES = 4
 ROWS_KIND, COLS_KIND, THIRD_KIND = 1, 2, 3
 OWN_ROW, OWN_COL, OWN_DIAG, OWN_GRAM = 1, 2, 3, 4
+CORES = 2
 
 
 def node(r, c):
@@ -61,20 +44,20 @@
             row_pairs.append((node(m, c), node(r, c)))
             top = max(r, c, m)
             kinds[node(r, c)] = [{r: ROWS_KIND, c: COLS_KIND, m: THIRD_KIND}[top], top]
-    diag_pairs, own = [], [0] * (BLOCKS**3)
+    diag_pairs, own = [[] for _ in range(PIECES)], [[0, 0]] * (BLOCKS**3)
     for d in range(BLOCKS):
+        grams = GRAM.get(d, ())
         for layer in range(BLOCKS):
-            own[device(layer, d, d)] = OWN_DIAG
-        for o in range(BLOCKS):
-            layer = PACKED_LAYER[d][o]
-            if layer >= 0:
-                target = device(layer, max(d, o), min(d, o))
-                diag_pairs.append((device(layer, d, d), target))
-                own[target] = OWN_COL if o > d else OWN_ROW
-            for layer in GRAM_LAYERS.get((d, o), ()):
-                target = device(layer, d, d)
-                diag_pairs.append((device(layer, o, d), target))
-                own[target] = OWN_GRAM
+            own[device(layer, d, d)] = [OWN_GRAM if grams else OWN_DIAG, 0]
+            for piece, o in enumerate(grams):
+                diag_pairs[piece].append((device(layer, o, d), device(layer, d, d)))
+        others = [o for o in range(BLOCKS) if o != d and o not in grams]
+        for i, o in enumerate(others):
+            for piece in range(PIECES):
+                chip = CORES * ((piece + i) % PIECES)
+                target = device(chip + (o < d), max(d, o), min(d, o))
+                diag_pairs[piece].append((device(chip + i // PIECES, d, d), target))
+                own[target] = [OWN_COL if o > d else OWN_ROW, piece]
     return col_pairs, row_pairs, diag_pairs, kinds, own
 
 
@@ -136,44 +119,51 @@
                 put(total, k * width)
 
 
-def own_kernel(info_ref, b_ref, u_ref, out_ref):
+def own_kernel(info_ref, b_ref, *refs):
+    u_refs, out_ref = refs[:-1], refs[-1]
     layer, r, c = (lax.axis_index(name) for name in ("layer", "row", "col"))
-    own, side = info_ref[(layer * BLOCKS + r) * BLOCKS + c], r - c
+    here = (layer * BLOCKS + r) * BLOCKS + c
+    own, piece, side = info_ref[2 * here], info_ref[2 * here + 1], r - c
     n = b_ref.shape[0]
     h = n // 2
     width = n // BLOCKS
     out_ref[...] = jnp.zeros_like(out_ref)
-    zero = jnp.zeros((), u_ref.dtype)
 
     def below(w, first_row):
         row = lax.broadcasted_iota(jnp.int32, w.shape, 0) + first_row
         col = lax.broadcasted_iota(jnp.int32, w.shape, 1)
         return jnp.where(row > col, w, jnp.zeros((), w.dtype))
 
-    def halves():
+    def parts(u_ref, first_row):
         mix = u_ref[:, h:]
-        row = lax.broadcasted_iota(jnp.int32, mix.shape, 0)
+        row = lax.broadcasted_iota(jnp.int32, mix.shape, 0) + first_row
         col = lax.broadcasted_iota(jnp.int32, mix.shape, 1)
+        zero = jnp.zeros((), mix.dtype)
         return u_ref[:, :h], jnp.where(row < col, mix, zero), jnp.where(row > col, mix, zero)
 
-    @pl.when(own == OWN_COL)
-    def _():
-        across, first, second = halves()
-        for s in range(0, n, STEP):
-            lo, hi = b_ref[s : s + STEP, :h], b_ref[s : s + STEP, h:]
-            p_lo = mm(hi, across) + mm(lo, first)
-            w = p_lo * lo.astype(F32) + mm(hi, second) * hi.astype(F32)
-            out_ref[0:1, s : s + STEP] = fold_lanes(w)
-
-    @pl.when(own == OWN_ROW)
-    def _():
-        across, first, second = halves()
-        for s in range(0, h, STEP):
-            p = mm(first[:, s : s + STEP], b_ref[:h, :], ((0,), (0,)))
-            out_ref[0:1, s : s + STEP] = fold_lanes(p * b_ref[s : s + STEP, :].astype(F32))
-        for s in range(0, h, STEP):
-            p = mm(across[s : s + STEP, :], b_ref[:h, :]) + mm(second[s : s + STEP, :], b_ref[h:, :])
-            out_ref[0:1, h + s : h + s + STEP] = fold_lanes(p * b_ref[h + s : h + s + STEP, :].astype(F32))
+    for k, u_ref in enumerate(u_refs):
+        step = u_ref.shape[0]
+        low, high = slice(k * step, (k + 1) * step), slice(h + k * step, h + (k + 1) * step)
+
+        @pl.when(jnp.logical_and(own == OWN_COL, piece == k))
+        def _(u_ref=u_ref, low=low, high=high, k=k, step=step):
+            across, first, second = parts(u_ref, k * step)
+            for s in range(0, n, STEP):
+                cut = slice(s, s + STEP)
+                lo, hi = b_ref[cut, low], b_ref[cut, high]
+                p_lo = mm(hi, across) + mm(lo, first)
+                w = p_lo * b_ref[cut, :h].astype(F32) + mm(hi, second) * b_ref[cut, h:].astype(F32)
+                out_ref[0:1, cut] = fold_lanes(w)
+
+        @pl.when(jnp.logical_and(own == OWN_ROW, piece == k))
+        def _(u_ref=u_ref, low=low, high=high, k=k, step=step):
+            across, first, second = parts(u_ref, k * step)
+            for s in range(0, h, STEP):
+                cut = slice(s, s + STEP)
+                p = mm(first[:, cut], b_ref[low, :], ((0,), (0,)))
+                out_ref[0:1, cut] = fold_lanes(p * b_ref[cut, :].astype(F32))
+            p = mm(across, b_ref[:h, :]) + mm(second, b_ref[h:, :])
+            out_ref[0:1, high] = fold_lanes(p * b_ref[high, :].astype(F32))
 
     for k in range(BLOCKS):
         cut = slice(k * width, (k + 1) * width)
@@ -195,12 +185,13 @@
                 out_ref[0:1, s : s + STEP] = fold_lanes(w)
 
 
-    @pl.when(own == OWN_GRAM)
-    def _():
-        for s in range(0, n, STEP):
-            e = s + STEP
-            g = mm(u_ref[:, s:e], u_ref[:, :e], ((0,), (0,)))
-            out_ref[0:1, s:e] += fold_lanes(g * below(b_ref[s:e, :e], s).astype(F32))
+    for k in range(max(len(o) for o in GRAM.values())):
+        @pl.when(own == OWN_GRAM)
+        def _(u_ref=u_refs[k]):
+            for s in range(0, n, STEP):
+                e = s + STEP
+                g = mm(u_ref[:, s:e], u_ref[:, :e], ((0,), (0,)))
+                out_ref[0:1, s:e] += fold_lanes(g * below(b_ref[s:e, :e], s).astype(F32))
 
 
 def cut_kernel(b_ref, columns_ref, rows_ref, sems):
@@ -216,27 +207,23 @@
         copy.wait()
 
 
-def pack_kernel(b_ref, out_ref):
-    h = out_ref.shape[0]
+def pack_kernel(b_ref, rows_ref, *out_refs):
+    h = b_ref.shape[0] // 2
     diagonal = lax.axis_index("row") == lax.axis_index("col")
-    second = lax.axis_index("layer") >= BLOCKS // 2
-
-    @pl.when(diagonal)
-    def _():
-        out_ref[:, :h] = b_ref[h:, :h]
-        row = lax.broadcasted_iota(jnp.int32, (h, h), 0)
-        col = lax.broadcasted_iota(jnp.int32, (h, h), 1)
-        out_ref[:, h:] = jnp.where(row > col, b_ref[h:, h:], b_ref[:h, :h])
-
-    @pl.when(jnp.logical_not(diagonal))
-    def _():
-        @pl.when(second)
-        def _():
-            out_ref[...] = b_ref[h:, :]
-
-        @pl.when(jnp.logical_not(second))
-        def _():
-            out_ref[...] = b_ref[:h, :]
+    for k, out_ref in enumerate(out_refs):
+        step = out_ref.shape[0]
+        low, high = slice(k * step, (k + 1) * step), slice(h + k * step, h + (k + 1) * step)
+
+        @pl.when(diagonal)
+        def _(out_ref=out_ref, low=low, high=high, k=k, step=step):
+            out_ref[:, :h] = b_ref[high, :h]
+            row = lax.broadcasted_iota(jnp.int32, (step, h), 0) + k * step
+            col = lax.broadcasted_iota(jnp.int32, (step, h), 1)
+            out_ref[:, h:] = jnp.where(row > col, b_ref[high, h:], b_ref[low, :h])
+
+        @pl.when(jnp.logical_not(diagonal))
+        def _(out_ref=out_ref):
+            out_ref[...] = rows_ref[...]
 
 
 def cut(edge_weight):
@@ -257,18 +244,19 @@
     )(edge_weight)
 
 
-def pack(edge_weight):
+def pack(edge_weight, rows):
     n = edge_weight.shape[0]
     whole = pl.BlockSpec(memory_space=pltpu.VMEM)
+    piece = jax.ShapeDtypeStruct((n // 2 // PIECES, n), edge_weight.dtype)
     return pl.pallas_call(
         pack_kernel,
-        out_shape=jax.ShapeDtypeStruct((n // 2, n), edge_weight.dtype),
-        in_specs=[whole],
-        out_specs=whole,
+        out_shape=(piece,) * PIECES,
+        in_specs=[whole, whole],
+        out_specs=(whole,) * PIECES,
         name="pack",
         cost_estimate=pl.CostEstimate(flops=0, bytes_accessed=2 * n * n, transcendentals=0),
         compiler_params=pltpu.CompilerParams(vmem_limit_bytes=16 * 1024 * 1024),
-    )(edge_weight)
+    )(edge_weight, rows)
 
 
 def vmem_call(kernel, out_shape, flops, nbytes):
@@ -289,24 +277,24 @@
 
 def step(edge_weight):
     n = edge_weight.shape[0]
-    width, half = n // BLOCKS, n // 2
+    width = n // BLOCKS
     col_pairs, row_pairs, diag_pairs, kinds, own = plan()
     triple_info = jnp.array(kinds, jnp.int32).reshape(-1)
-    own_info = jnp.array(own, jnp.int32)
+    own_info = jnp.array(own, jnp.int32).reshape(-1)
 
     columns, rows = cut(edge_weight)
     x = lax.ppermute(columns, ("row", "col"), col_pairs)
     z = lax.ppermute(rows, ("row", "col"), row_pairs)
-    packed = pack(edge_weight)
-    u = lax.ppermute(packed, ("layer", "row", "col"), diag_pairs)
+    packed = pack(edge_weight, rows)
+    u = [lax.ppermute(p, ("layer", "row", "col"), pairs) for p, pairs in zip(packed, diag_pairs)]
 
     triples = vmem_call(
         triple_kernel, jax.ShapeDtypeStruct((BLOCKS, n), F32), 2 * n * n * width, 2 * n * n
     )(triple_info, edge_weight, x, z)
     back = lax.all_to_all(triples, "row", 0, 0, tiled=True)
     mine = vmem_call(
-        own_kernel, jax.ShapeDtypeStruct((2, n), F32), 3 * n * n * half, 4 * n * n
-    )(own_info, edge_weight, u)
+        own_kernel, jax.ShapeDtypeStruct((2, n), F32), n * n * n // 2, 4 * n * n
+    )(own_info, edge_weight, *u)
     total = jnp.sum(back, axis=0) + mine[0]
     peers = BLOCKS * BLOCKS
     sent = jnp.stack([total.reshape(peers, n // peers), mine[1].reshape(peers, n // peers)], axis=1)

time: 74.4 us -> 70.2 us (0.944)
  blocking collectives: 54.2 us -> 15.1 us
  starting transfers between devices: 13.9 us -> 43.1 us
  waiting for transfers between devices: 0.01 us -> 4.8 us
    all_to_all x1 -> x0, blocking collectives: 32.9 us -> none  [step(): back = lax.all_to_all(triples, 'row', 0, 0, tiled=True)]
    all_to_all x0 -> x1, starting transfers between devices: none -> 15.7 us  [step(): back = lax.all_to_all(triples, 'row', 0, 0, tiled=True)]
    ppermute x1 -> x4, starting transfers between devices: 12.5 us -> 26 us  [step(): lax.ppermute(p, ('layer', 'row', 'col'), pairs)]
    all_to_all x1, blocking collectives: 21.3 us -> 15.1 us  [step(): lax.all_to_all(sent, ('layer', 'col'), 0, 0, tiled=True)]
    all_to_all x0 -> x1, waiting for transfers between devices: none -> 4.79 us  [step(): back = lax.all_to_all(triples, 'row', 0, 0, tiled=True)]
    pallas_call x1, Pallas kernels: 0.1 us -> 1.02 us  [pack(): pl.pallas_call(pack_kernel, out_shape=(piece,) * PIECES, in_specs=[whole,...]
  transfers between devices with their start and end apart: 3 -> 7, of which waited for: 0 -> 1; matrix products, arithmetic and copies ran while one was open for 0% -> 1% of each run, Pallas kernels for 1% -> 5%
where the time goes in v4:
time: 70.2 us; the launch traced here: 69.9 us
  starting transfers between devices  43.1 us (61%)
  blocking collectives  15.1 us (22%)
  waiting for transfers between devices  4.8 us (7%)
  Pallas kernels  3.55 us (5%)
  local copies, waits for them, and re-layouts  2.54 us (4%)
    ppermute x4, starting transfers between devices, step(): lax.ppermute(p, ('layer', 'row', 'col'), pairs)  26 us
    all_to_all x1, starting transfers between devices, step(): back = lax.all_to_all(triples, 'row', 0, 0, tiled=True)  15.7 us
    all_to_all x1, blocking collectives, step(): lax.all_to_all(sent, ('layer', 'col'), 0, 0, tiled=True)  15.1 us
    all_to_all x1, waiting for transfers between devices, step(): back = lax.all_to_all(triples, 'row', 0, 0, tiled=True)  4.79 us
    pallas_call x2, Pallas kernels, call(): pl.pallas_call(kernel, out_shape=out_shape, in_specs=[pl.BlockSpec(memory...  2.43 us
    unnamed x8, local copies, waits for them, and re-layouts  1.6 us
  transfers between devices with their start and end apart: 7, of which 1 were waited for; matrix products, arithmetic and copies ran while one was open for 1% of the time, Pallas kernels for 5%

profile of v4, /device:TPU:1, one launch (start us, length us, event | category | flops | bytes accessed | tf_op | source)
XLA Modules:
  0.0 69.9 jit_solution(2231928577304255336)
XLA Ops:
  0.0 0.0 copy-start
  0.0 1.6 %copy-done = bf16[1024,1024]{1,0:T(8,128)(2,1)S(1)} copy-done((bf16[1024,1024]{1,0:T(8,128)(2,1)S(1)}, bf16[1024,1024]{1,0:T(8,128)(2,1)}, u32[]{:S(2)}) %copy-start) | copy-done | bytes 2097176
  1.6 0.1 cut.1
  1.7 0.8 %collective-permute-start = (bf16[1024,128]{1,0:T(8,128)(2,1)S(1)}, bf16[1024,128]{1,0:T(8,128)(2,1)S(1)}, u32[]{:S(2)}, u32[]{:S(2)}) collective-permute-start(bf16[1024,128]{1,0:T(8,128)(2,1)S(1)} %get-tuple-element.11), channel_id=1, source_target_pairs={{3,1},{6,2},{4,3},{2,4},{7,5},{5,6},{1,7},{12,8},{8,10},{13,11},{1... | collective-permute-start | bytes 786440 | tf_op jit(solution)/shard_map/ppermute | solution.py:286
  2.5 0.0 copy-start.2
  2.5 0.7 collective-permute-start.1
  3.2 0.0 copy-done.1
  3.2 1.0 %pack.1 = (bf16[128,1024]{1,0:T(8,128)(2,1)}, bf16[128,1024]{1,0:T(8,128)(2,1)}, bf16[128,1024]{1,0:T(8,128)(2,1)}, bf16[128,1024]{1,0:T(8,128)(2,1)S(1)}) custom-call(bf16[1024,1024]{1,0:T(8,128)(2,1)S(1)} %copy-done.1, bf16[128,1024]{1,0:T(8,128)(2,1)S(1)} %get-tuple-element.12.rows_ref), custom_call_target="tpu_custom_call" | custom-call | bytes 2097152 | tf_op jit(solution)/shard_map/pack/pallas_call | solution.py:251
  4.3 21.2 %collective-permute-start.2 = (bf16[128,1024]{1,0:T(8,128)(2,1)}, bf16[128,1024]{1,0:T(8,128)(2,1)S(1)}, u32[]{:S(2)}, u32[]{:S(2)}) collective-permute-start(bf16[128,1024]{1,0:T(8,128)(2,1)} %get-tuple-element.13), channel_id=1, source_target_pairs={{0,8},{128,144},{256,280},{384,416},{64,40},{192,176},{320,312},{9... | collective-permute-start | bytes 786440 | tf_op jit(solution)/shard_map/ppermute | solution.py:289
  25.5 0.7 collective-permute-start.3
  26.2 2.8 %collective-permute-start.4 = (bf16[128,1024]{1,0:T(8,128)(2,1)}, bf16[128,1024]{1,0:T(8,128)(2,1)S(1)}, u32[]{:S(2)}, u32[]{:S(2)}) collective-permute-start(bf16[128,1024]{1,0:T(8,128)(2,1)} %get-tuple-element.15), channel_id=1, source_target_pairs={{256,264},{384,400},{0,24},{128,160},{320,296},{448,432},{64,56},{... | collective-permute-start | bytes 786440 | tf_op jit(solution)/shard_map/ppermute | solution.py:289
  28.9 0.0 collective-permute-done.x_ref
  28.9 1.3 %collective-permute-start.5 = (bf16[128,1024]{1,0:T(8,128)(2,1)S(1)}, bf16[128,1024]{1,0:T(8,128)(2,1)S(1)}, u32[]{:S(2)}, u32[]{:S(2)}) collective-permute-start(bf16[128,1024]{1,0:T(8,128)(2,1)S(1)} %get-tuple-element.16), channel_id=1, source_target_pairs={{384,392},{0,16},{128,152},{256,288},{448,424},{64,48},{192,184},{... | collective-permute-start | bytes 786440 | tf_op jit(solution)/shard_map/ppermute | solution.py:289
  30.3 0.0 collective-permute-done.1.z_ref
  30.3 0.0 copy-done.3
  30.3 0.6 shard_map.37
  30.9 0.6 copy.8
  31.5 15.7 %all-to-all-start = ((f32[8,1,1024]{2,1,0:T(1,128)}), f32[8,1,1024]{2,1,0:T(1,128)S(1)}, u32[]{:S(2)}, u32[]{:S(2)}) async-start(f32[8,1,1024]{2,1,0:T(1,128)} %copy.8), calls=%async_computation | async-start | bytes 65536 | tf_op jit(solution)/shard_map/all_to_all | solution.py:294
  47.1 0.0 collective-permute-done.2.refs_0_
  47.2 0.0 collective-permute-done.3.refs_1_
  47.2 0.0 collective-permute-done.4.refs_2_
  47.2 0.0 collective-permute-done.5.refs_3_
  47.2 0.0 copy-done.2
  47.2 1.9 %shard_map.38 = f32[2,1024]{1,0:T(2,128)S(1)} custom-call(s32[1024]{0:T(1024)S(1)} %copy-done.2, bf16[1024,1024]{1,0:T(8,128)(2,1)S(1)} %copy-done.1, bf16[128,1024]{1,0:T(8,128)(2,1)S(1)} %collective-permute-done.2.refs_0_, bf16[128,1024]{1,0:T(8,128)(2,1)S(1)} %collective-permute-done.3.refs_1_, bf16[128,1024]{1,0:T(8,128)(2,1)S(1)} %collective-permute-done.4.refs_2_, ...), custom_call_target="tpu_custom_call" | custom-call | flops 536870912 | bytes 4194304 | tf_op jit(solution)/shard_map/pallas_call | solution.py:266
  49.1 0.1 squeeze.2
  49.2 0.1 stack_reshape_squeeze.3
  49.2 4.8 %all-to-all-done = f32[8,1,1024]{2,1,0:T(1,128)S(1)} async-done(((f32[8,1,1024]{2,1,0:T(1,128)}), f32[8,1,1024]{2,1,0:T(1,128)S(1)}, u32[]{:S(2)}, u32[]{:S(2)}) %all-to-all-start) | async-done | bytes 32800 | tf_op jit(solution)/shard_map/all_to_all | solution.py:294
  54.1 0.1 reduce_sum.21
  54.2 0.1 copy.9
  54.2 15.1 %all_to_all.14 = f32[64,2,16]{2,1,0:T(2,128)S(1)} all-to-all(f32[64,2,16]{2,1,0:T(2,128)S(1)} %copy.9), channel_id=1, replica_groups=mesh['layer'=8,'row'=8,'col'=8] {'layer','col'}, dimensions={0} | all-to-all | bytes 16384 | tf_op jit(solution)/shard_map/all_to_all | solution.py:301
  69.3 0.1 reduce_sum.22
  69.4 0.5 fusion.1
  (6 shorter events, 0.1 us)
Async XLA Ops:
  0.0 1.6 %copy-start = (bf16[1024,1024]{1,0:T(8,128)(2,1)S(1)}, bf16[1024,1024]{1,0:T(8,128)(2,1)}, u32[]{:S(2)}) copy-start(bf16[1024,1024]{1,0:T(8,128)(2,1)} %b_ref.7) | copy-start | bytes 6291460
  1.6 1.6 %copy-start.1 = (bf16[1024,1024]{1,0:T(8,128)(2,1)S(1)}, bf16[1024,1024]{1,0:T(8,128)(2,1)}, u32[]{:S(2)}) copy-start(bf16[1024,1024]{1,0:T(8,128)(2,1)} %b_ref.7) | copy-start | bytes 6291460
  1.6 28.7 %copy-start.3 = (s32[128]{0:T(128)S(1)}, s32[128]{0:T(128)}, u32[]{:S(2)}) copy-start(s32[128]{0:T(128)} %constant.13.info_ref) | copy-start | bytes 1540
  1.7 27.2 %collective-permute-start = (bf16[1024,128]{1,0:T(8,128)(2,1)S(1)}, bf16[1024,128]{1,0:T(8,128)(2,1)S(1)}, u32[]{:S(2)}, u32[]{:S(2)}) collective-permute-start(bf16[1024,128]{1,0:T(8,128)(2,1)S(1)} %get-tuple-element.11), channel_id=1, source_target_pairs={{3,1},{6,2},{4,3},{2,4},{7,5},{5,6},{1,7},{12,8},{8,10},{13,11},{1... | collective-permute-start | bytes 786440 | tf_op jit(solution)/shard_map/ppermute | solution.py:286
  2.5 44.7 %copy-start.2 = (s32[1024]{0:T(1024)S(1)}, s32[1024]{0:T(1024)}, u32[]{:S(2)}) copy-start(s32[1024]{0:T(1024)} %constant.14.info_ref) | copy-start | bytes 12292
  2.5 27.7 %collective-permute-start.1 = (bf16[128,1024]{1,0:T(8,128)(2,1)S(1)}, bf16[128,1024]{1,0:T(8,128)(2,1)S(1)}, u32[]{:S(2)}, u32[]{:S(2)}) collective-permute-start(bf16[128,1024]{1,0:T(8,128)(2,1)S(1)} %get-tuple-element.12.rows_ref), channel_id=1, source_target_pairs={{25,1},{50,2},{35,3},{20,4},{61,5},{46,6},{15,7},{32,8},{2,10},{43... | collective-permute-start | bytes 786440 | tf_op jit(solution)/shard_map/ppermute | solution.py:287
  4.3 42.9 %collective-permute-start.2 = (bf16[128,1024]{1,0:T(8,128)(2,1)}, bf16[128,1024]{1,0:T(8,128)(2,1)S(1)}, u32[]{:S(2)}, u32[]{:S(2)}) collective-permute-start(bf16[128,1024]{1,0:T(8,128)(2,1)} %get-tuple-element.13), channel_id=1, source_target_pairs={{0,8},{128,144},{256,280},{384,416},{64,40},{192,176},{320,312},{9... | collective-permute-start | bytes 786440 | tf_op jit(solution)/shard_map/ppermute | solution.py:289
  25.5 21.7 %collective-permute-start.3 = (bf16[128,1024]{1,0:T(8,128)(2,1)}, bf16[128,1024]{1,0:T(8,128)(2,1)S(1)}, u32[]{:S(2)}, u32[]{:S(2)}) collective-permute-start(bf16[128,1024]{1,0:T(8,128)(2,1)} %get-tuple-element.14), channel_id=1, source_target_pairs={{128,136},{256,272},{384,408},{0,32},{192,168},{320,304},{448,440}... | collective-permute-start | bytes 786440 | tf_op jit(solution)/shard_map/ppermute | solution.py:289
  26.2 21.0 %collective-permute-start.4 = (bf16[128,1024]{1,0:T(8,128)(2,1)}, bf16[128,1024]{1,0:T(8,128)(2,1)S(1)}, u32[]{:S(2)}, u32[]{:S(2)}) collective-permute-start(bf16[128,1024]{1,0:T(8,128)(2,1)} %get-tuple-element.15), channel_id=1, source_target_pairs={{256,264},{384,400},{0,24},{128,160},{320,296},{448,432},{64,56},{... | collective-permute-start | bytes 786440 | tf_op jit(solution)/shard_map/ppermute | solution.py:289
  28.9 18.2 %collective-permute-start.5 = (bf16[128,1024]{1,0:T(8,128)(2,1)S(1)}, bf16[128,1024]{1,0:T(8,128)(2,1)S(1)}, u32[]{:S(2)}, u32[]{:S(2)}) collective-permute-start(bf16[128,1024]{1,0:T(8,128)(2,1)S(1)} %get-tuple-element.16), channel_id=1, source_target_pairs={{384,392},{0,16},{128,152},{256,288},{448,424},{64,48},{192,184},{... | collective-permute-start | bytes 786440 | tf_op jit(solution)/shard_map/ppermute | solution.py:289
  31.5 22.5 %all-to-all-start = ((f32[8,1,1024]{2,1,0:T(1,128)}), f32[8,1,1024]{2,1,0:T(1,128)S(1)}, u32[]{:S(2)}, u32[]{:S(2)}) async-start(f32[8,1,1024]{2,1,0:T(1,128)} %copy.8), calls=%async_computation | async-start | bytes 65536 | tf_op jit(solution)/shard_map/all_to_all | solution.py:294

commit v5 on v4

--- a/solution.py
+++ b/solution.py
@@ -77,6 +77,7 @@
 
 
 STEP = 256
+LANES = 128
 
 
 def triple_kernel(info_ref, b_ref, x_ref, z_ref, out_ref):
@@ -86,10 +87,8 @@
     out_ref[...] = jnp.zeros_like(out_ref)
 
     def put(vector, start):
-        shape = (out_ref.shape[0], vector.shape[1])
-        row = lax.broadcasted_iota(jnp.int32, shape, 0)
-        spread = jnp.broadcast_to(vector, shape)
-        out_ref[:, start : start + shape[1]] = jnp.where(row == top, spread, jnp.zeros_like(spread))
+        for t in range(vector.shape[1] // LANES):
+            out_ref[top, start // LANES + t, :] = vector[0, t * LANES : (t + 1) * LANES]
 
     @pl.when(kind == ROWS_KIND)
     def _():
@@ -286,16 +285,18 @@
     x = lax.ppermute(columns, ("row", "col"), col_pairs)
     z = lax.ppermute(rows, ("row", "col"), row_pairs)
     packed = pack(edge_weight, rows)
-    u = [lax.ppermute(p, ("layer", "row", "col"), pairs) for p, pairs in zip(packed, diag_pairs)]
+    u = []
+    for piece, pairs in enumerate(diag_pairs):
+        u.append(lax.ppermute(packed[piece], ("layer", "row", "col"), pairs))
 
     triples = vmem_call(
-        triple_kernel, jax.ShapeDtypeStruct((BLOCKS, n), F32), 2 * n * n * width, 2 * n * n
+        triple_kernel, jax.ShapeDtypeStruct((BLOCKS, n // LANES, LANES), F32), 2 * n * n * width, 2 * n * n
     )(triple_info, edge_weight, x, z)
     back = lax.all_to_all(triples, "row", 0, 0, tiled=True)
     mine = vmem_call(
         own_kernel, jax.ShapeDtypeStruct((2, n), F32), n * n * n // 2, 4 * n * n
     )(own_info, edge_weight, *u)
-    total = jnp.sum(back, axis=0) + mine[0]
+    total = jnp.sum(back, axis=0).reshape(n) + mine[0]
     peers = BLOCKS * BLOCKS
     sent = jnp.stack([total.reshape(peers, n // peers), mine[1].reshape(peers, n // peers)], axis=1)
     got = jnp.sum(lax.all_to_all(sent, ("layer", "col"), 0, 0, tiled=True), axis=0)

time: 70.2 us -> 70.2 us (level)
  transfers between devices with their start and end apart: 7 -> 7, of which waited for: 1 -> 1; matrix products, arithmetic and copies ran while one was open for 1% -> 0% of each run, Pallas kernels for 5% -> 6%
where the time goes in v5:
time: 70.2 us; the launch traced here: 69.9 us
  starting transfers between devices  43.1 us (61%)
  blocking collectives  15.1 us (22%)
  waiting for transfers between devices  4.8 us (7%)
  Pallas kernels  4.15 us (6%)
  local copies, waits for them, and re-layouts  1.9 us (3%)
    ppermute x4, starting transfers between devices, step(): u.append(lax.ppermute(packed[piece], ('layer', 'row', 'col'), pairs))  26 us
    all_to_all x1, starting transfers between devices, step(): back = lax.all_to_all(triples, 'row', 0, 0, tiled=True)  15.7 us
    all_to_all x1, blocking collectives, step(): lax.all_to_all(sent, ('layer', 'col'), 0, 0, tiled=True)  15.1 us
    all_to_all x1, waiting for transfers between devices, step(): back = lax.all_to_all(triples, 'row', 0, 0, tiled=True)  4.79 us
    pallas_call x2, Pallas kernels, call(): pl.pallas_call(kernel, out_shape=out_shape, in_specs=[pl.BlockSpec(memory...  3.03 us
    unnamed x8, local copies, waits for them, and re-layouts  1.6 us
  transfers between devices with their start and end apart: 7, of which 1 were waited for; matrix products, arithmetic and copies ran while one was open for 0% of the time, Pallas kernels for 6%

profile of v5, /device:TPU:1, one launch (start us, length us, event | category | flops | bytes accessed | tf_op | source)
XLA Modules:
  0.0 69.9 jit_solution(1008985968761257435)
XLA Ops:
  0.0 0.0 copy-start
  0.0 1.6 %copy-done = bf16[1024,1024]{1,0:T(8,128)(2,1)S(1)} copy-done((bf16[1024,1024]{1,0:T(8,128)(2,1)S(1)}, bf16[1024,1024]{1,0:T(8,128)(2,1)}, u32[]{:S(2)}) %copy-start) | copy-done | bytes 2097176
  1.6 0.0 copy-start.1
  1.6 0.1 cut.1
  1.7 0.8 %collective-permute-start = (bf16[1024,128]{1,0:T(8,128)(2,1)S(1)}, bf16[1024,128]{1,0:T(8,128)(2,1)S(1)}, u32[]{:S(2)}, u32[]{:S(2)}) collective-permute-start(bf16[1024,128]{1,0:T(8,128)(2,1)S(1)} %get-tuple-element.11), channel_id=1, source_target_pairs={{3,1},{6,2},{4,3},{2,4},{7,5},{5,6},{1,7},{12,8},{8,10},{13,11},{1... | collective-permute-start | bytes 786440 | tf_op jit(solution)/shard_map/ppermute | solution.py:285
  2.5 0.0 copy-start.2
  2.5 0.7 collective-permute-start.1
  3.2 0.0 copy-done.1
  3.2 1.0 %pack.1 = (bf16[128,1024]{1,0:T(8,128)(2,1)}, bf16[128,1024]{1,0:T(8,128)(2,1)}, bf16[128,1024]{1,0:T(8,128)(2,1)}, bf16[128,1024]{1,0:T(8,128)(2,1)S(1)}) custom-call(bf16[1024,1024]{1,0:T(8,128)(2,1)S(1)} %copy-done.1, bf16[128,1024]{1,0:T(8,128)(2,1)S(1)} %get-tuple-element.12.rows_ref), custom_call_target="tpu_custom_call" | custom-call | bytes 2097152 | tf_op jit(solution)/shard_map/pack/pallas_call | solution.py:250
  4.3 21.2 %collective-permute-start.2 = (bf16[128,1024]{1,0:T(8,128)(2,1)}, bf16[128,1024]{1,0:T(8,128)(2,1)S(1)}, u32[]{:S(2)}, u32[]{:S(2)}) collective-permute-start(bf16[128,1024]{1,0:T(8,128)(2,1)} %get-tuple-element.13), channel_id=1, source_target_pairs={{0,8},{128,144},{256,280},{384,416},{64,40},{192,176},{320,312},{9... | collective-permute-start | bytes 786440 | tf_op jit(solution)/shard_map/ppermute | solution.py:290
  25.5 0.7 collective-permute-start.3
  26.2 2.8 %collective-permute-start.4 = (bf16[128,1024]{1,0:T(8,128)(2,1)}, bf16[128,1024]{1,0:T(8,128)(2,1)S(1)}, u32[]{:S(2)}, u32[]{:S(2)}) collective-permute-start(bf16[128,1024]{1,0:T(8,128)(2,1)} %get-tuple-element.15), channel_id=1, source_target_pairs={{256,264},{384,400},{0,24},{128,160},{320,296},{448,432},{64,56},{... | collective-permute-start | bytes 786440 | tf_op jit(solution)/shard_map/ppermute | solution.py:290
  28.9 0.0 collective-permute-done.x_ref
  28.9 1.3 %collective-permute-start.5 = (bf16[128,1024]{1,0:T(8,128)(2,1)S(1)}, bf16[128,1024]{1,0:T(8,128)(2,1)S(1)}, u32[]{:S(2)}, u32[]{:S(2)}) collective-permute-start(bf16[128,1024]{1,0:T(8,128)(2,1)S(1)} %get-tuple-element.16), channel_id=1, source_target_pairs={{384,392},{0,16},{128,152},{256,288},{448,424},{64,48},{192,184},{... | collective-permute-start | bytes 786440 | tf_op jit(solution)/shard_map/ppermute | solution.py:290
  30.3 0.0 collective-permute-done.1.z_ref
  30.3 0.0 copy-done.3
  30.3 1.2 %shard_map.37 = f32[8,8,128]{2,1,0:T(8,128)} custom-call(s32[128]{0:T(128)S(1)} %copy-done.3, bf16[1024,1024]{1,0:T(8,128)(2,1)S(1)} %copy-done.1, bf16[1024,128]{1,0:T(8,128)(2,1)S(1)} %collective-permute-done.x_ref, bf16[128,1024]{1,0:T(8,128)(2,1)S(1)} %collective-permute-done.1.z_ref), custom_call_target="tpu_custom_call" | custom-call | flops 268435456 | bytes 2097152 | tf_op jit(solution)/shard_map/pallas_call | solution.py:265
  31.4 15.7 %all-to-all-start = ((f32[8,8,128]{2,1,0:T(8,128)}), f32[8,8,128]{2,1,0:T(8,128)S(1)}, u32[]{:S(2)}, u32[]{:S(2)}) async-start(f32[8,8,128]{2,1,0:T(8,128)} %shard_map.37), calls=%async_computation | async-start | bytes 65536 | tf_op jit(solution)/shard_map/all_to_all | solution.py:295
  47.1 0.0 collective-permute-done.2.refs_0_
  47.1 0.0 collective-permute-done.3.refs_1_
  47.1 0.0 collective-permute-done.4.refs_2_
  47.1 0.0 collective-permute-done.5.refs_3_
  47.1 0.0 copy-done.2
  47.2 1.9 %shard_map.38 = f32[2,1024]{1,0:T(2,128)S(1)} custom-call(s32[1024]{0:T(1024)S(1)} %copy-done.2, bf16[1024,1024]{1,0:T(8,128)(2,1)S(1)} %copy-done.1, bf16[128,1024]{1,0:T(8,128)(2,1)S(1)} %collective-permute-done.2.refs_0_, bf16[128,1024]{1,0:T(8,128)(2,1)S(1)} %collective-permute-done.3.refs_1_, bf16[128,1024]{1,0:T(8,128)(2,1)S(1)} %collective-permute-done.4.refs_2_, ...), custom_call_target="tpu_custom_call" | custom-call | flops 536870912 | bytes 4194304 | tf_op jit(solution)/shard_map/pallas_call | solution.py:265
  49.1 0.1 squeeze.2
  49.1 0.1 stack_reshape_squeeze.3
  49.2 4.8 %all-to-all-done = f32[8,8,128]{2,1,0:T(8,128)S(1)} async-done(((f32[8,8,128]{2,1,0:T(8,128)}), f32[8,8,128]{2,1,0:T(8,128)S(1)}, u32[]{:S(2)}, u32[]{:S(2)}) %all-to-all-start) | async-done | bytes 32800 | tf_op jit(solution)/shard_map/all_to_all | solution.py:295
  54.0 0.1 reshape.28
  54.1 0.1 copy.7
  54.2 15.1 %all_to_all.10 = f32[64,2,16]{2,1,0:T(2,128)S(1)} all-to-all(f32[64,2,16]{2,1,0:T(2,128)S(1)} %copy.7), channel_id=1, replica_groups=mesh['layer'=8,'row'=8,'col'=8] {'layer','col'}, dimensions={0} | all-to-all | bytes 16384 | tf_op jit(solution)/shard_map/all_to_all | solution.py:302
  69.2 0.1 reduce_sum.19
  69.3 0.5 fusion.1
  (5 shorter events, 0.1 us)
Async XLA Ops:
  0.0 1.6 %copy-start = (bf16[1024,1024]{1,0:T(8,128)(2,1)S(1)}, bf16[1024,1024]{1,0:T(8,128)(2,1)}, u32[]{:S(2)}) copy-start(bf16[1024,1024]{1,0:T(8,128)(2,1)} %b_ref.7) | copy-start | bytes 6291460
  1.6 1.6 %copy-start.1 = (bf16[1024,1024]{1,0:T(8,128)(2,1)S(1)}, bf16[1024,1024]{1,0:T(8,128)(2,1)}, u32[]{:S(2)}) copy-start(bf16[1024,1024]{1,0:T(8,128)(2,1)} %b_ref.7) | copy-start | bytes 6291460
  1.6 28.7 %copy-start.3 = (s32[128]{0:T(128)S(1)}, s32[128]{0:T(128)}, u32[]{:S(2)}) copy-start(s32[128]{0:T(128)} %constant.13.info_ref) | copy-start | bytes 1540
  1.7 27.2 %collective-permute-start = (bf16[1024,128]{1,0:T(8,128)(2,1)S(1)}, bf16[1024,128]{1,0:T(8,128)(2,1)S(1)}, u32[]{:S(2)}, u32[]{:S(2)}) collective-permute-start(bf16[1024,128]{1,0:T(8,128)(2,1)S(1)} %get-tuple-element.11), channel_id=1, source_target_pairs={{3,1},{6,2},{4,3},{2,4},{7,5},{5,6},{1,7},{12,8},{8,10},{13,11},{1... | collective-permute-start | bytes 786440 | tf_op jit(solution)/shard_map/ppermute | solution.py:285
  2.5 44.6 %copy-start.2 = (s32[1024]{0:T(1024)S(1)}, s32[1024]{0:T(1024)}, u32[]{:S(2)}) copy-start(s32[1024]{0:T(1024)} %constant.14.info_ref) | copy-start | bytes 12292
  2.5 27.7 %collective-permute-start.1 = (bf16[128,1024]{1,0:T(8,128)(2,1)S(1)}, bf16[128,1024]{1,0:T(8,128)(2,1)S(1)}, u32[]{:S(2)}, u32[]{:S(2)}) collective-permute-start(bf16[128,1024]{1,0:T(8,128)(2,1)S(1)} %get-tuple-element.12.rows_ref), channel_id=1, source_target_pairs={{25,1},{50,2},{35,3},{20,4},{61,5},{46,6},{15,7},{32,8},{2,10},{43... | collective-permute-start | bytes 786440 | tf_op jit(solution)/shard_map/ppermute | solution.py:286
  4.3 42.9 %collective-permute-start.2 = (bf16[128,1024]{1,0:T(8,128)(2,1)}, bf16[128,1024]{1,0:T(8,128)(2,1)S(1)}, u32[]{:S(2)}, u32[]{:S(2)}) collective-permute-start(bf16[128,1024]{1,0:T(8,128)(2,1)} %get-tuple-element.13), channel_id=1, source_target_pairs={{0,8},{128,144},{256,280},{384,416},{64,40},{192,176},{320,312},{9... | collective-permute-start | bytes 786440 | tf_op jit(solution)/shard_map/ppermute | solution.py:290
  25.5 21.6 %collective-permute-start.3 = (bf16[128,1024]{1,0:T(8,128)(2,1)}, bf16[128,1024]{1,0:T(8,128)(2,1)S(1)}, u32[]{:S(2)}, u32[]{:S(2)}) collective-permute-start(bf16[128,1024]{1,0:T(8,128)(2,1)} %get-tuple-element.14), channel_id=1, source_target_pairs={{128,136},{256,272},{384,408},{0,32},{192,168},{320,304},{448,440}... | collective-permute-start | bytes 786440 | tf_op jit(solution)/shard_map/ppermute | solution.py:290
  26.2 21.0 %collective-permute-start.4 = (bf16[128,1024]{1,0:T(8,128)(2,1)}, bf16[128,1024]{1,0:T(8,128)(2,1)S(1)}, u32[]{:S(2)}, u32[]{:S(2)}) collective-permute-start(bf16[128,1024]{1,0:T(8,128)(2,1)} %get-tuple-element.15), channel_id=1, source_target_pairs={{256,264},{384,400},{0,24},{128,160},{320,296},{448,432},{64,56},{... | collective-permute-start | bytes 786440 | tf_op jit(solution)/shard_map/ppermute | solution.py:290
  28.9 18.2 %collective-permute-start.5 = (bf16[128,1024]{1,0:T(8,128)(2,1)S(1)}, bf16[128,1024]{1,0:T(8,128)(2,1)S(1)}, u32[]{:S(2)}, u32[]{:S(2)}) collective-permute-start(bf16[128,1024]{1,0:T(8,128)(2,1)S(1)} %get-tuple-element.16), channel_id=1, source_target_pairs={{384,392},{0,16},{128,152},{256,288},{448,424},{64,48},{192,184},{... | collective-permute-start | bytes 786440 | tf_op jit(solution)/shard_map/ppermute | solution.py:290
  31.4 22.5 %all-to-all-start = ((f32[8,8,128]{2,1,0:T(8,128)}), f32[8,8,128]{2,1,0:T(8,128)S(1)}, u32[]{:S(2)}, u32[]{:S(2)}) async-start(f32[8,8,128]{2,1,0:T(8,128)} %shard_map.37), calls=%async_computation | async-start | bytes 65536 | tf_op jit(solution)/shard_map/all_to_all | solution.py:295

commit v6 on v5

--- a/solution.py
+++ b/solution.py
@@ -9,16 +9,16 @@
 F32 = jnp.float32
 BLOCKS = 8
 THIRD = [
-    [0, 3, 6, 4, 2, 7, 5, 1],
-    [4, 1, 0, 5, 3, 6, 7, 2],
-    [5, 6, 2, 1, 7, 4, 3, 0],
-    [2, 7, 5, 3, 6, 0, 1, 4],
-    [7, 5, 1, 2, 4, 3, 0, 6],
-    [1, 2, 7, 6, 0, 5, 4, 3],
-    [3, 0, 4, 7, 1, 2, 6, 5],
-    [6, 4, 3, 0, 5, 1, 2, 7],
+    [0, 2, 6, 5, 3, 7, 4, 1],
+    [3, 1, 7, 2, 6, 4, 0, 5],
+    [5, 4, 2, 7, 0, 1, 3, 6],
+    [2, 5, 4, 3, 1, 6, 7, 0],
+    [1, 7, 5, 6, 4, 0, 2, 3],
+    [6, 0, 3, 4, 7, 5, 1, 2],
+    [7, 3, 1, 0, 5, 2, 6, 4],
+    [4, 6, 0, 1, 2, 3, 5, 7],
 ]
-GRAM = {4: (0, 1), 5: (0, 2), 6: (0, 3), 7: (0, 3)}
+GRAM = {4: (0, 3), 5: (0, 3), 6: (0, 3), 7: (0, 2)}
 PIECES = 4
 ROWS_KIND, COLS_KIND, THIRD_KIND = 1, 2, 3
 OWN_ROW, OWN_COL, OWN_DIAG, OWN_GRAM = 1, 2, 3, 4

time: 70.2 us -> 68.7 us (0.979)
  starting transfers between devices: 43.1 us -> 31.7 us
  blocking collectives: 15.1 us -> 25.1 us
    all_to_all x1, starting transfers between devices: 15.7 us -> 4.27 us  [step(): back = lax.all_to_all(triples, 'row', 0, 0, tiled=True)]
    all_to_all x1, blocking collectives: 15.1 us -> 25.1 us  [step(): lax.all_to_all(sent, ('layer', 'col'), 0, 0, tiled=True)]
where the time goes in v6:
time: 68.7 us; the launch traced here: 68.4 us
  starting transfers between devices  31.7 us (46%)
  blocking collectives  25.1 us (37%)
  waiting for transfers between devices  4.8 us (7%)
  Pallas kernels  4.15 us (6%)
  local copies, waits for them, and re-layouts  1.9 us (3%)
    ppermute x4, starting transfers between devices, step(): u.append(lax.ppermute(packed[piece], ('layer', 'row', 'col'), pairs))  25.9 us
    all_to_all x1, blocking collectives, step(): lax.all_to_all(sent, ('layer', 'col'), 0, 0, tiled=True)  25.1 us
    all_to_all x1, waiting for transfers between devices, step(): back = lax.all_to_all(triples, 'row', 0, 0, tiled=True)  4.79 us
    all_to_all x1, starting transfers between devices, step(): back = lax.all_to_all(triples, 'row', 0, 0, tiled=True)  4.27 us
    pallas_call x2, Pallas kernels, call(): pl.pallas_call(kernel, out_shape=out_shape, in_specs=[pl.BlockSpec(memory...  3.03 us
    unnamed x8, local copies, waits for them, and re-layouts  1.6 us
  transfers between devices with their start and end apart: 7, of which 1 were waited for; matrix products, arithmetic and copies ran while one was open for 0% of the time, Pallas kernels for 6%

profile of v6, /device:TPU:1, one launch (start us, length us, event | category | flops | bytes accessed | tf_op | source)
XLA Modules:
  0.0 68.4 jit_solution(11647923695732756229)
XLA Ops:
  0.0 0.0 copy-start
  0.0 1.6 %copy-done = bf16[1024,1024]{1,0:T(8,128)(2,1)S(1)} copy-done((bf16[1024,1024]{1,0:T(8,128)(2,1)S(1)}, bf16[1024,1024]{1,0:T(8,128)(2,1)}, u32[]{:S(2)}) %copy-start) | copy-done | bytes 2097176
  1.6 0.0 copy-start.1
  1.6 0.1 cut.1
  1.7 0.8 %collective-permute-start = (bf16[1024,128]{1,0:T(8,128)(2,1)S(1)}, bf16[1024,128]{1,0:T(8,128)(2,1)S(1)}, u32[]{:S(2)}, u32[]{:S(2)}) collective-permute-start(bf16[1024,128]{1,0:T(8,128)(2,1)S(1)} %get-tuple-element.11), channel_id=1, source_target_pairs={{2,1},{6,2},{5,3},{3,4},{7,5},{4,6},{1,7},{11,8},{15,10},{10,11},{... | collective-permute-start | bytes 786440 | tf_op jit(solution)/shard_map/ppermute | solution.py:285
  2.5 0.0 copy-start.2
  2.5 0.7 collective-permute-start.1
  3.2 0.0 copy-done.1
  3.2 1.0 %pack.1 = (bf16[128,1024]{1,0:T(8,128)(2,1)}, bf16[128,1024]{1,0:T(8,128)(2,1)}, bf16[128,1024]{1,0:T(8,128)(2,1)}, bf16[128,1024]{1,0:T(8,128)(2,1)S(1)}) custom-call(bf16[1024,1024]{1,0:T(8,128)(2,1)S(1)} %copy-done.1, bf16[128,1024]{1,0:T(8,128)(2,1)S(1)} %get-tuple-element.12.rows_ref), custom_call_target="tpu_custom_call" | custom-call | bytes 2097152 | tf_op jit(solution)/shard_map/pack/pallas_call | solution.py:250
  4.3 19.0 %collective-permute-start.2 = (bf16[128,1024]{1,0:T(8,128)(2,1)}, bf16[128,1024]{1,0:T(8,128)(2,1)S(1)}, u32[]{:S(2)}, u32[]{:S(2)}) collective-permute-start(bf16[128,1024]{1,0:T(8,128)(2,1)} %get-tuple-element.13), channel_id=1, source_target_pairs={{0,8},{128,144},{256,280},{384,416},{64,40},{192,176},{320,312},{9... | collective-permute-start | bytes 786440 | tf_op jit(solution)/shard_map/ppermute | solution.py:290
  23.3 0.7 collective-permute-start.3
  24.0 1.3 %collective-permute-start.4 = (bf16[128,1024]{1,0:T(8,128)(2,1)}, bf16[128,1024]{1,0:T(8,128)(2,1)S(1)}, u32[]{:S(2)}, u32[]{:S(2)}) collective-permute-start(bf16[128,1024]{1,0:T(8,128)(2,1)} %get-tuple-element.15), channel_id=1, source_target_pairs={{256,264},{384,400},{0,24},{128,160},{320,296},{448,432},{64,56},{... | collective-permute-start | bytes 786440 | tf_op jit(solution)/shard_map/ppermute | solution.py:290
  25.3 0.0 collective-permute-done.x_ref
  25.3 4.9 %collective-permute-start.5 = (bf16[128,1024]{1,0:T(8,128)(2,1)S(1)}, bf16[128,1024]{1,0:T(8,128)(2,1)S(1)}, u32[]{:S(2)}, u32[]{:S(2)}) collective-permute-start(bf16[128,1024]{1,0:T(8,128)(2,1)S(1)} %get-tuple-element.16), channel_id=1, source_target_pairs={{384,392},{0,16},{128,152},{256,288},{448,424},{64,48},{192,184},{... | collective-permute-start | bytes 786440 | tf_op jit(solution)/shard_map/ppermute | solution.py:290
  30.2 0.0 collective-permute-done.1.z_ref
  30.2 0.0 copy-done.3
  30.2 1.2 %shard_map.37 = f32[8,8,128]{2,1,0:T(8,128)} custom-call(s32[128]{0:T(128)S(1)} %copy-done.3, bf16[1024,1024]{1,0:T(8,128)(2,1)S(1)} %copy-done.1, bf16[1024,128]{1,0:T(8,128)(2,1)S(1)} %collective-permute-done.x_ref, bf16[128,1024]{1,0:T(8,128)(2,1)S(1)} %collective-permute-done.1.z_ref), custom_call_target="tpu_custom_call" | custom-call | flops 268435456 | bytes 2097152 | tf_op jit(solution)/shard_map/pallas_call | solution.py:265
  31.4 4.3 %all-to-all-start = ((f32[8,8,128]{2,1,0:T(8,128)}), f32[8,8,128]{2,1,0:T(8,128)S(1)}, u32[]{:S(2)}, u32[]{:S(2)}) async-start(f32[8,8,128]{2,1,0:T(8,128)} %shard_map.37), calls=%async_computation | async-start | bytes 65536 | tf_op jit(solution)/shard_map/all_to_all | solution.py:295
  35.7 0.0 collective-permute-done.2.refs_0_
  35.7 0.0 collective-permute-done.3.refs_1_
  35.7 0.0 collective-permute-done.4.refs_2_
  35.7 0.0 collective-permute-done.5.refs_3_
  35.7 0.0 copy-done.2
  35.7 1.9 %shard_map.38 = f32[2,1024]{1,0:T(2,128)S(1)} custom-call(s32[1024]{0:T(1024)S(1)} %copy-done.2, bf16[1024,1024]{1,0:T(8,128)(2,1)S(1)} %copy-done.1, bf16[128,1024]{1,0:T(8,128)(2,1)S(1)} %collective-permute-done.2.refs_0_, bf16[128,1024]{1,0:T(8,128)(2,1)S(1)} %collective-permute-done.3.refs_1_, bf16[128,1024]{1,0:T(8,128)(2,1)S(1)} %collective-permute-done.4.refs_2_, ...), custom_call_target="tpu_custom_call" | custom-call | flops 536870912 | bytes 4194304 | tf_op jit(solution)/shard_map/pallas_call | solution.py:265
  37.6 0.1 squeeze.2
  37.7 0.1 stack_reshape_squeeze.3
  37.8 4.8 %all-to-all-done = f32[8,8,128]{2,1,0:T(8,128)S(1)} async-done(((f32[8,8,128]{2,1,0:T(8,128)}), f32[8,8,128]{2,1,0:T(8,128)S(1)}, u32[]{:S(2)}, u32[]{:S(2)}) %all-to-all-start) | async-done | bytes 32800 | tf_op jit(solution)/shard_map/all_to_all | solution.py:295
  42.6 0.1 reshape.28
  42.7 0.1 copy.7
  42.7 25.1 %all_to_all.10 = f32[64,2,16]{2,1,0:T(2,128)S(1)} all-to-all(f32[64,2,16]{2,1,0:T(2,128)S(1)} %copy.7), channel_id=1, replica_groups=mesh['layer'=8,'row'=8,'col'=8] {'layer','col'}, dimensions={0} | all-to-all | bytes 16384 | tf_op jit(solution)/shard_map/all_to_all | solution.py:302
  67.8 0.1 reduce_sum.19
  67.9 0.5 fusion.1
  (5 shorter events, 0.1 us)
Async XLA Ops:
  0.0 1.6 %copy-start = (bf16[1024,1024]{1,0:T(8,128)(2,1)S(1)}, bf16[1024,1024]{1,0:T(8,128)(2,1)}, u32[]{:S(2)}) copy-start(bf16[1024,1024]{1,0:T(8,128)(2,1)} %b_ref.7) | copy-start | bytes 6291460
  1.6 1.6 %copy-start.1 = (bf16[1024,1024]{1,0:T(8,128)(2,1)S(1)}, bf16[1024,1024]{1,0:T(8,128)(2,1)}, u32[]{:S(2)}) copy-start(bf16[1024,1024]{1,0:T(8,128)(2,1)} %b_ref.7) | copy-start | bytes 6291460
  1.6 28.6 %copy-start.3 = (s32[128]{0:T(128)S(1)}, s32[128]{0:T(128)}, u32[]{:S(2)}) copy-start(s32[128]{0:T(128)} %constant.13.info_ref) | copy-start | bytes 1540
  1.7 23.6 %collective-permute-start = (bf16[1024,128]{1,0:T(8,128)(2,1)S(1)}, bf16[1024,128]{1,0:T(8,128)(2,1)S(1)}, u32[]{:S(2)}, u32[]{:S(2)}) collective-permute-start(bf16[1024,128]{1,0:T(8,128)(2,1)S(1)} %get-tuple-element.11), channel_id=1, source_target_pairs={{2,1},{6,2},{5,3},{3,4},{7,5},{4,6},{1,7},{11,8},{15,10},{10,11},{... | collective-permute-start | bytes 786440 | tf_op jit(solution)/shard_map/ppermute | solution.py:285
  2.5 33.2 %copy-start.2 = (s32[1024]{0:T(1024)S(1)}, s32[1024]{0:T(1024)}, u32[]{:S(2)}) copy-start(s32[1024]{0:T(1024)} %constant.14.info_ref) | copy-start | bytes 12292
  2.5 27.7 %collective-permute-start.1 = (bf16[128,1024]{1,0:T(8,128)(2,1)S(1)}, bf16[128,1024]{1,0:T(8,128)(2,1)S(1)}, u32[]{:S(2)}, u32[]{:S(2)}) collective-permute-start(bf16[128,1024]{1,0:T(8,128)(2,1)S(1)} %get-tuple-element.12.rows_ref), channel_id=1, source_target_pairs={{17,1},{50,2},{43,3},{28,4},{61,5},{38,6},{15,7},{24,8},{58,10},{1... | collective-permute-start | bytes 786440 | tf_op jit(solution)/shard_map/ppermute | solution.py:286
  4.3 31.4 %collective-permute-start.2 = (bf16[128,1024]{1,0:T(8,128)(2,1)}, bf16[128,1024]{1,0:T(8,128)(2,1)S(1)}, u32[]{:S(2)}, u32[]{:S(2)}) collective-permute-start(bf16[128,1024]{1,0:T(8,128)(2,1)} %get-tuple-element.13), channel_id=1, source_target_pairs={{0,8},{128,144},{256,280},{384,416},{64,40},{192,176},{320,312},{9... | collective-permute-start | bytes 786440 | tf_op jit(solution)/shard_map/ppermute | solution.py:290
  23.3 12.4 %collective-permute-start.3 = (bf16[128,1024]{1,0:T(8,128)(2,1)}, bf16[128,1024]{1,0:T(8,128)(2,1)S(1)}, u32[]{:S(2)}, u32[]{:S(2)}) collective-permute-start(bf16[128,1024]{1,0:T(8,128)(2,1)} %get-tuple-element.14), channel_id=1, source_target_pairs={{128,136},{256,272},{384,408},{0,32},{192,168},{320,304},{448,440}... | collective-permute-start | bytes 786440 | tf_op jit(solution)/shard_map/ppermute | solution.py:290
  24.0 11.7 %collective-permute-start.4 = (bf16[128,1024]{1,0:T(8,128)(2,1)}, bf16[128,1024]{1,0:T(8,128)(2,1)S(1)}, u32[]{:S(2)}, u32[]{:S(2)}) collective-permute-start(bf16[128,1024]{1,0:T(8,128)(2,1)} %get-tuple-element.15), channel_id=1, source_target_pairs={{256,264},{384,400},{0,24},{128,160},{320,296},{448,432},{64,56},{... | collective-permute-start | bytes 786440 | tf_op jit(solution)/shard_map/ppermute | solution.py:290
  25.3 10.4 %collective-permute-start.5 = (bf16[128,1024]{1,0:T(8,128)(2,1)S(1)}, bf16[128,1024]{1,0:T(8,128)(2,1)S(1)}, u32[]{:S(2)}, u32[]{:S(2)}) collective-permute-start(bf16[128,1024]{1,0:T(8,128)(2,1)S(1)} %get-tuple-element.16), channel_id=1, source_target_pairs={{384,392},{0,16},{128,152},{256,288},{448,424},{64,48},{192,184},{... | collective-permute-start | bytes 786440 | tf_op jit(solution)/shard_map/ppermute | solution.py:290
  31.4 11.1 %all-to-all-start = ((f32[8,8,128]{2,1,0:T(8,128)}), f32[8,8,128]{2,1,0:T(8,128)S(1)}, u32[]{:S(2)}, u32[]{:S(2)}) async-start(f32[8,8,128]{2,1,0:T(8,128)} %shard_map.37), calls=%async_computation | async-start | bytes 65536 | tf_op jit(solution)/shard_map/all_to_all | solution.py:295
